TPU v7x, 32 devices: a whole 2x2x4 slice. The times are simulated.
32 devices in a mesh: dp: 4 (over z), fsdp: 8 (over y, x, core).
Axes of the slice: x: 2, y: 2, z: 4, core: 2. Of those that a mesh axis runs over, the one named last changes fastest.
Arguments:
- x_in: bfloat16 [128, 384, 1536], P(('dp', 'fsdp'))
- positions: int32 [128, 384], P(('dp', 'fsdp'))
- segments: int32 [128, 384], P(('dp', 'fsdp'))
- rel_bias: float32 [32, 16], replicated
- gain_attn: float32 [1536], replicated
- gain_mlp: float32 [1536], replicated
- w_q: bfloat16 [1536, 1024], P('fsdp')
- w_k: bfloat16 [1536, 1024], P('fsdp')
- w_v: bfloat16 [1536, 1024], P('fsdp')
- w_o: bfloat16 [1024, 1536], P('fsdp')
- w_i0: bfloat16 [1536, 3840], P('fsdp')
- w_i1: bfloat16 [1536, 3840], P('fsdp')
- w_f: bfloat16 [3840, 1536], P('fsdp')
- grad_out: bfloat16 [128, 384, 1536], P(('dp', 'fsdp'))
Outputs:
- output 1: bfloat16 [128, 384, 1536], P(('dp', 'fsdp'))
- output 2: float32 [32, 16], replicated
- output 3: float32 [1536], replicated
- output 4: float32 [1536], replicated
- output 5: bfloat16 [1536, 1024], P('fsdp')
- output 6: bfloat16 [1536, 1024], P('fsdp')
- output 7: bfloat16 [1536, 1024], P('fsdp')
- output 8: bfloat16 [1024, 1536], P('fsdp')
- output 9: bfloat16 [1536, 3840], P('fsdp')
- output 10: bfloat16 [1536, 3840], P('fsdp')
- output 11: bfloat16 [3840, 1536], P('fsdp')
All inputs are finite; a program needn't handle non-finite values.
Results may differ from a plain program's by a relative error of at most 0.0194871.
Values are sent between devices in bfloat16 or wider.
A program may use at most 1 GiB of HBM per device.

v0:
```python
import jax
import jax.numpy as jnp
from jax import lax
from jax.sharding import PartitionSpec as P

EPSILON = 1e-6
NEG_BIG = -1e9
REL_CLASSES = 32
HALF_CLASSES = 16
EXACT_RANGE = 8
THRESHOLDS = (12, 16, 23, 32, 46, 64, 91)
ROW_AXES = ('dp', 'fsdp')


def rms_norm(values, gain):
    inv_rms = lax.rsqrt(jnp.mean(values * values, axis=-1, keepdims=True) + EPSILON)
    return (values * inv_rms * gain).astype(jnp.bfloat16)


def class_onehot(positions):
    offset = positions[:, None, :] - positions[:, :, None]
    distance = jnp.abs(offset)
    magnitude = jnp.minimum(distance, EXACT_RANGE)
    for bound in THRESHOLDS:
        magnitude = magnitude + (distance >= bound).astype(jnp.int32)
    rel_cls = magnitude + HALF_CLASSES * (offset > 0).astype(jnp.int32)
    return (rel_cls[..., None] == jnp.arange(REL_CLASSES, dtype=jnp.int32)).astype(jnp.float32)


def segment_mask(segments):
    same_seg = segments[:, :, None] == segments[:, None, :]
    return jnp.where(same_seg, 0.0, NEG_BIG).astype(jnp.float32)


def project(tokens_in, weight):
    return jnp.einsum('rsd,de->rse', tokens_in, weight, preferred_element_type=jnp.float32)


def attn_forward(q_all, k_all, v_all, onehot, mask_add, rel_bias):
    bias = jnp.einsum('rqkc,ch->hrqk', onehot, rel_bias, precision=lax.Precision.HIGHEST)
    scores = jnp.einsum('rqhd,rkhd->hrqk', q_all, k_all, preferred_element_type=jnp.float32) + bias + mask_add
    attn_prob = jax.nn.softmax(scores, axis=-1)
    context = jnp.einsum('hrqk,rkhd->rqhd', attn_prob.astype(jnp.bfloat16), v_all, preferred_element_type=jnp.float32)
    return context.astype(jnp.bfloat16), attn_prob


def attn_backward(d_context, q_all, k_all, v_all, attn_prob, onehot):
    prob_low = attn_prob.astype(jnp.bfloat16)
    d_v = jnp.einsum('hrqk,rqhd->rkhd', prob_low, d_context, preferred_element_type=jnp.float32).astype(jnp.bfloat16)
    d_prob = jnp.einsum('rqhd,rkhd->hrqk', d_context, v_all, preferred_element_type=jnp.float32)
    d_scores = attn_prob * (d_prob - jnp.sum(d_prob * attn_prob, axis=-1, keepdims=True))
    d_bias = jnp.einsum('hrqk,rqkc->ch', d_scores, onehot, precision=lax.Precision.HIGHEST)
    d_low = d_scores.astype(jnp.bfloat16)
    d_q = jnp.einsum('hrqk,rkhd->rqhd', d_low, k_all, preferred_element_type=jnp.float32).astype(jnp.bfloat16)
    d_k = jnp.einsum('hrqk,rqhd->rkhd', d_low, q_all, preferred_element_type=jnp.float32).astype(jnp.bfloat16)
    return d_q, d_k, d_v, d_bias


def gather_full(part):
    return lax.all_gather(part, 'fsdp', axis=0, tiled=True)


def reduce_weight(full_grad):
    shard = lax.psum_scatter(full_grad, 'fsdp', scatter_dimension=0, tiled=True)
    return lax.psum(shard, 'dp').astype(jnp.bfloat16)


def local_layer(x_in, positions, segments, rel_bias, gain_attn, gain_mlp, wq_part, wk_part, wv_part, wo_part, wi0_part, wi1_part, wf_part, grad_out):
    w_q = gather_full(wq_part)
    w_k = gather_full(wk_part)
    w_v = gather_full(wv_part)
    w_o = gather_full(wo_part)
    w_i0 = gather_full(wi0_part)
    w_i1 = gather_full(wi1_part)
    w_f = gather_full(wf_part)
    rows, seq_len = x_in.shape[0], x_in.shape[1]
    heads = rel_bias.shape[1]
    x_float = x_in.astype(jnp.float32)
    normed, norm1_pull = jax.vjp(lambda gain: rms_norm(x_float, gain), gain_attn)
    q_all = project(normed, w_q).astype(jnp.bfloat16).reshape(rows, seq_len, heads, -1)
    k_all = project(normed, w_k).astype(jnp.bfloat16).reshape(rows, seq_len, heads, -1)
    v_all = project(normed, w_v).astype(jnp.bfloat16).reshape(rows, seq_len, heads, -1)
    onehot = class_onehot(positions)
    mask_add = segment_mask(segments)
    context, attn_prob = attn_forward(q_all, k_all, v_all, onehot, mask_add, rel_bias)
    context = context.reshape(rows, seq_len, -1)
    hidden = (x_float + project(context, w_o)).astype(jnp.bfloat16)
    h_float = hidden.astype(jnp.float32)
    mlp_in, norm2_pull = jax.vjp(rms_norm, h_float, gain_mlp)
    gate = project(mlp_in, w_i0)
    up_proj = project(mlp_in, w_i1)
    act_float, act_pull = jax.vjp(lambda gate_in, up_in: jax.nn.silu(gate_in) * up_in, gate, up_proj)
    hidden_act = act_float.astype(jnp.bfloat16)
    y_out = (h_float + project(hidden_act, w_f)).astype(jnp.bfloat16)

    d_act = jnp.einsum('rsd,fd->rsf', grad_out, w_f, preferred_element_type=jnp.float32).astype(jnp.bfloat16)
    d_wf = jnp.einsum('rsf,rsd->fd', hidden_act, grad_out, preferred_element_type=jnp.float32)
    d_gate, d_up = act_pull(d_act.astype(jnp.float32))
    d_gate = d_gate.astype(jnp.bfloat16)
    d_up = d_up.astype(jnp.bfloat16)
    d_wi0 = jnp.einsum('rsd,rsf->df', mlp_in, d_gate, preferred_element_type=jnp.float32)
    d_wi1 = jnp.einsum('rsd,rsf->df', mlp_in, d_up, preferred_element_type=jnp.float32)
    d_mlp_in = (jnp.einsum('rsf,df->rsd', d_gate, w_i0, preferred_element_type=jnp.float32)
                + jnp.einsum('rsf,df->rsd', d_up, w_i1, preferred_element_type=jnp.float32)).astype(jnp.bfloat16)
    d_h_norm, d_gain_mlp = norm2_pull(d_mlp_in)
    d_hidden = (grad_out.astype(jnp.float32) + d_h_norm).astype(jnp.bfloat16)
    d_wo = jnp.einsum('rse,rsd->ed', context, d_hidden, preferred_element_type=jnp.float32)
    d_context = jnp.einsum('rsd,ed->rse', d_hidden, w_o, preferred_element_type=jnp.float32).astype(jnp.bfloat16).reshape(rows, seq_len, heads, -1)
    d_q, d_k, d_v, d_bias = attn_backward(d_context, q_all, k_all, v_all, attn_prob, onehot)
    d_q = d_q.reshape(rows, seq_len, -1)
    d_k = d_k.reshape(rows, seq_len, -1)
    d_v = d_v.reshape(rows, seq_len, -1)
    d_wq = jnp.einsum('rsd,rse->de', normed, d_q, preferred_element_type=jnp.float32)
    d_wk = jnp.einsum('rsd,rse->de', normed, d_k, preferred_element_type=jnp.float32)
    d_wv = jnp.einsum('rsd,rse->de', normed, d_v, preferred_element_type=jnp.float32)
    d_normed = (jnp.einsum('rse,de->rsd', d_q, w_q, preferred_element_type=jnp.float32)
                + jnp.einsum('rse,de->rsd', d_k, w_k, preferred_element_type=jnp.float32)
                + jnp.einsum('rse,de->rsd', d_v, w_v, preferred_element_type=jnp.float32)).astype(jnp.bfloat16)
    d_gain_attn = norm1_pull(d_normed)[0]
    return (y_out, lax.psum(d_bias, ROW_AXES), lax.psum(d_gain_attn, ROW_AXES), lax.psum(d_gain_mlp, ROW_AXES),
            reduce_weight(d_wq), reduce_weight(d_wk), reduce_weight(d_wv), reduce_weight(d_wo),
            reduce_weight(d_wi0), reduce_weight(d_wi1), reduce_weight(d_wf))


def solution(mesh):
    row_spec = P(ROW_AXES)
    whole = P()
    part_spec = P('fsdp')
    in_specs = (row_spec, row_spec, row_spec, whole, whole, whole) + (part_spec,) * 7 + (row_spec,)
    out_specs = (row_spec, whole, whole, whole) + (part_spec,) * 7
    return jax.shard_map(local_layer, mesh=mesh, in_specs=in_specs, out_specs=out_specs, check_vma=False)
```

profile of v0, /device:TPU:0, one launch (start us, length us, event | category | flops | bytes accessed | tf_op | source)
XLA Modules:
  0.0 1605.5 jit_solution(2007262197941877531)
XLA Ops:
  7.2 0.7 all-gather.10.cloned.1.call-update
  8.0 0.7 all-gather.12.cloned.1.call-update
  8.7 0.7 all-gather.8.cloned.1.call-update
  9.5 0.5 all-gather.14.cloned.1.call-update
  10.1 0.5 all-gather.20.cloned.1.call-update
  10.6 0.5 all-gather.18.cloned.1.call-update
  11.2 0.7 all-gather.16.cloned.1.call-update
  12.0 3.3 fusion.39
  15.5 4.9 fusion.89
  20.7 1.1 copy-done.2
  21.8 26.4 %fusion.1 = f32[4,384,384,16]{1,3,2,0:T(8,128)} fusion(f32[32,16]{0,1:T(8,128)S(1)} %copy-done, s32[4,384,384]{1,0,2:T(4,128)S(1)} %fusion.89), kind=kOutput, calls=%fused_computation.2 | convolution fusion | flops 3642753024 | bytes 40110080 | tf_op jit(solution)/shard_map/rqkc,ch->hrqk/dot_general | solution.py:40
  48.1 9.6 fusion.93
  57.7 4.7 copy.55
  62.4 16.6 %all-gather.12.cloned.1.call-done = bf16[1536,1024]{1,0:T(8,128)(2,1)} async-done(((bf16[192,1024]{1,0:T(8,128)(2,1)}), bf16[1536,1024]{1,0:T(8,128)(2,1)}) %all-gather.12.cloned.1.call-update) | async-done | bytes 3145744 | tf_op jit(solution)/shard_map/all_gather | solution.py:60
  78.9 9.9 fusion.96
  88.8 4.6 copy.56
  93.5 19.6 %all-gather.8.cloned.1.call-done = bf16[1536,1024]{1,0:T(8,128)(2,1)} async-done(((bf16[192,1024]{1,0:T(8,128)(2,1)}), bf16[1536,1024]{1,0:T(8,128)(2,1)}) %all-gather.8.cloned.1.call-update) | async-done | bytes 3145744 | tf_op jit(solution)/shard_map/all_gather | solution.py:60
  113.0 9.6 fusion.90
  122.6 4.7 copy.54
  127.3 36.7 %fusion.131 = (f32[16,4,384]{2,1,0:T(4,128)S(1)}, f32[16,4,384,384]{2,3,1,0:T(8,128)}) fusion(f32[4,384,384,16]{1,3,2,0:T(8,128)} %fusion.1, f32[4,384,384]{1,2,0:T(8,128)S(1)} %compare_select_fusion, bf16[4,384,16,64]{1,3,2,0:T(8,128)(2,1)} %bitcast.124, bf16[4,384,16,64]{1,3,2,0:T(8,128)(2,1)} %bitcast.126), kind=kOutput, calls=%fused_computation.132 | convolution fusion | flops 1245708672 | bytes 84246528 | tf_op jit(solution)/shard_map/sub | solution.py:42
  164.1 23.1 %fusion.129 = bf16[16,4,384,384]{2,3,1,0:T(8,128)(2,1)} fusion(f32[16,4,384,384]{2,3,1,0:T(8,128)} %get-tuple-element.29, f32[16,4,384]{2,1,0:T(4,128)S(1)} %get-tuple-element.28), kind=kLoop, calls=%fused_computation.130 | loop fusion | flops 18874368 | bytes 56721408 | tf_op jit(solution)/shard_map/convert_element_type | solution.py:43
  187.1 11.5 fusion.102
  198.7 10.8 fusion.43
  209.5 0.6 copy-done.14
  210.1 7.3 all-gather.20.cloned.1.call-done
  217.4 24.5 %fusion.46 = bf16[4,384,3840]{2,1,0:T(8,128)(2,1)} fusion(bf16[4,384,1536]{2,1,0:T(8,128)(2,1)} %param.27, bf16[3840,1536]{1,0:T(8,128)(2,1)} %all-gather.20.cloned.1.call-done), kind=kOutput, calls=%fused_computation.73 | convolution fusion | flops 18125291520 | bytes 28311552 | tf_op jit(solution)/shard_map/rsd,fd->rsf/dot_general | solution.py:96
  241.9 45.9 %all-gather.18.cloned.1.call-done = bf16[1536,3840]{1,0:T(8,128)(2,1)} async-done(((bf16[192,3840]{1,0:T(8,128)(2,1)}), bf16[1536,3840]{1,0:T(8,128)(2,1)}) %all-gather.18.cloned.1.call-update) | async-done | bytes 11796496 | tf_op jit(solution)/shard_map/all_gather | solution.py:60
  287.9 25.8 %fusion.25 = f32[4,384,3840]{2,1,0:T(8,128)} fusion(bf16[1536,3840]{1,0:T(8,128)(2,1)} %all-gather.18.cloned.1.call-done, bf16[4,384,1536]{2,1,0:T(8,128)(2,1)} %get-tuple-element.31, f32[1536]{0:T(1024)S(1)} %copy-done.17, f32[4,384]{1,0:T(4,128)S(1)} %fusion.122), kind=kOutput, calls=%fused_computation.48 | convolution fusion | flops 18128830464 | bytes 40120320 | tf_op jit(solution)/shard_map/rsd,de->rse/dot_general | solution.py:36
  313.7 44.8 %all-gather.16.cloned.1.call-done = bf16[1536,3840]{1,0:T(8,128)(2,1)} async-done(((bf16[192,3840]{1,0:T(8,128)(2,1)}), bf16[1536,3840]{1,0:T(8,128)(2,1)}) %all-gather.16.cloned.1.call-update) | async-done | bytes 11796496 | tf_op jit(solution)/shard_map/all_gather | solution.py:60
  358.5 39.5 %fusion.9 = (bf16[4,384,3840]{2,1,0:T(8,128)(2,1)}, bf16[4,384,3840]{2,1,0:T(8,128)(2,1)}, bf16[4,384,3840]{2,1,0:T(8,128)(2,1)}) fusion(f32[4,384,3840]{2,1,0:T(8,128)} %fusion.25, bf16[4,384,3840]{2,1,0:T(8,128)(2,1)} %fusion.46, bf16[1536,3840]{1,0:T(8,128)(2,1)} %all-gather.16.cloned.1.call-done, bf16[4,384,1536]{2,1,0:T(8,128)(2,1)} %get-tuple-element.31, ...), kind=kOutput, calls=%fused_computation.17 | convolution fusion | flops 18229100544 | bytes 87306240 | tf_op jit(solution)/shard_map/rsd,de->rse/dot_general | solution.py:36
  397.9 26.4 %fusion.23 = f32[4,384,1536]{2,1,0:T(8,128)} fusion(bf16[4,384,3840]{2,1,0:T(8,128)(2,1)} %get-tuple-element.27, bf16[1536,3840]{1,0:T(8,128)(2,1)} %all-gather.18.cloned.1.call-done), kind=kOutput, calls=%fused_computation.46 | convolution fusion | flops 18119393280 | bytes 33030144 | tf_op jit(solution)/shard_map/rsf,df->rsd/dot_general | solution.py:104
  424.3 28.8 %fusion.38 = (f32[1536]{0:T(1024)}, f32[4,384]{1,0:T(4,128)S(1)}, bf16[4,384,1536]{2,1,0:T(8,128)(2,1)}) fusion(bf16[4,384,1536]{2,1,0:T(8,128)(2,1)} %get-tuple-element.31, f32[4,384]{1,0:T(4,128)S(1)} %fusion.122, f32[1536]{0:T(1024)S(1)} %copy-done.17, f32[4,384,1536]{2,1,0:T(8,128)} %fusion.23, bf16[4,384,3840]{2,1,0:T(8,128)(2,1)} %get-tuple-element.25, ...), kind=kOutput, calls=%fused_computation.63 | convolution fusion | flops 18142982144 | bytes 42491904 | tf_op jit(solution)/shard_map/rsf,df->rsd/dot_general | solution.py:103
  453.1 7.2 fusion.42
  460.3 2.2 copy-done.6
  462.6 7.0 convolution_bitcast_fusion.3
  469.7 1.8 copy-done.25
  471.5 8.8 fusion.99
  480.3 5.1 copy.64
  485.4 12.4 fusion.105
  497.8 9.7 convolution_bitcast_fusion.4
  507.5 1.8 copy-done.8
  509.4 26.4 %multiply_reduce_fusion = (f32[16,4,384]{2,1,0:T(4,128)S(1)}, f32[16,4,384,384]{2,3,1,0:T(8,128)}) fusion(f32[16,4,384,384]{2,3,1,0:T(8,128)} %get-tuple-element.29, f32[16,4,384]{2,1,0:T(4,128)S(1)} %copy-done.10, bf16[4,384,16,64]{1,3,2,0:T(8,128)(2,1)S(1)} %bitcast.133, bf16[4,384,16,64]{1,3,2,0:T(8,128)(2,1)} %bitcast.135), kind=kOutput, calls=%fused_computation.9 | convolution fusion | flops 1236246528 | bytes 81985536 | tf_op jit(solution)/shard_map/rqhd,rkhd->hrqk/dot_general | solution.py:50
  535.8 48.7 %fusion.130 = (bf16[16,4,384,384]{2,3,1,0:T(8,128)(2,1)}, f32[16,4,384,384]{2,3,1,0:T(8,128)}) fusion(f32[16,4,384,384]{2,3,1,0:T(8,128)} %get-tuple-element.34, f32[16,4,384]{2,1,0:T(4,128)S(1)} %get-tuple-element.33, f32[16,4,384,384]{2,3,1,0:T(8,128)} %get-tuple-element.29, f32[16,4,384]{2,1,0:T(4,128)S(1)} %copy-done.10), kind=kLoop, calls=%fused_computation.131 | loop fusion | flops 37748736 | bytes 132317184 | tf_op jit(solution)/shard_map/convert_element_type | solution.py:53
  584.5 10.7 fusion.111
  595.3 1.6 copy-done.29
  596.9 10.1 convolution_bitcast_fusion.5
  607.1 1.8 copy-done.4
  608.9 12.0 fusion.108
  620.8 11.3 convolution_bitcast_fusion.6
  632.2 26.0 %convolution_bitcast_fusion.2 = f32[3840,1536]{1,0:T(8,128)} fusion(bf16[4,384,3840]{2,1,0:T(8,128)(2,1)} %get-tuple-element.26, bf16[4,384,1536]{2,1,0:T(8,128)(2,1)} %param.27), kind=kOutput, calls=%fused_computation.29 | convolution fusion | flops 18119393280 | bytes 40108032 | tf_op jit(solution)/shard_map/rsf,rsd->fd/dot_general | solution.py:97
  658.3 0.6 copy-done.13
  658.9 27.2 %convolution_bitcast_fusion = f32[1536,3840]{1,0:T(8,128)} fusion(bf16[4,384,3840]{2,1,0:T(8,128)(2,1)} %get-tuple-element.27, bf16[4,384,1536]{2,1,0:T(8,128)(2,1)} %get-tuple-element.31, f32[1536]{0:T(1024)S(1)} %copy-done.18, f32[4,384]{1,0:T(4,128)S(1)} %copy-done.13), kind=kOutput, calls=%fused_computation.27 | convolution fusion | flops 18128830464 | bytes 40120320 | tf_op jit(solution)/shard_map/rsd,rsf->df/dot_general | solution.py:102
  686.2 27.2 %convolution_bitcast_fusion.1 = f32[1536,3840]{1,0:T(8,128)} fusion(bf16[4,384,3840]{2,1,0:T(8,128)(2,1)} %get-tuple-element.25, bf16[4,384,1536]{2,1,0:T(8,128)(2,1)} %get-tuple-element.31, f32[1536]{0:T(1024)S(1)} %copy-done.18, f32[4,384]{1,0:T(4,128)S(1)} %copy-done.13), kind=kOutput, calls=%fused_computation.28 | convolution fusion | flops 18128830464 | bytes 40120320 | tf_op jit(solution)/shard_map/rsd,rsf->df/dot_general | solution.py:101
  713.5 1.9 copy-done.23
  715.4 9.6 fusion.64
  725.0 7.7 fusion.68
  732.7 12.0 fusion.37
  744.7 61.2 %fusion.118 = f32[32,16]{0,1:T(8,128)S(1)} fusion(f32[16,4,384,384]{2,3,1,0:T(8,128)} %get-tuple-element.24, s32[4,384,384]{1,0,2:T(4,128)S(1)} %copy-done.3), kind=kOutput, calls=%fused_computation.124 | convolution fusion | flops 3642753024 | bytes 40110080 | tf_op jit(solution)/shard_map/hrqk,rqkc->ch/dot_general | solution.py:52
  805.9 41.9 %all-reduce = (f32[32,16]{0,1:T(8,128)}, f32[1536]{0:T(1024)}, f32[1536]{0:T(1024)}) all-reduce(f32[32,16]{0,1:T(8,128)S(1)} %fusion.118, f32[1536]{0:T(1024)S(1)} %fusion.37, f32[1536]{0:T(1024)S(1)} %copy-done.19), channel_id=1, replica_groups=mesh['dp'=4,'fsdp'=8] {'dp','fsdp'}, use_global_device_ids=true, to_apply=%region_6.7 | all-reduce | flops 3584 | bytes 28672 | tf_op jit(solution)/shard_map/psum | solution.py:120
  847.8 25.8 %fusion.44 = bf16[4,384,1536]{2,1,0:T(8,128)(2,1)} fusion(bf16[4,384,1536]{2,1,0:T(8,128)(2,1)} %get-tuple-element.31, bf16[4,384,3840]{2,1,0:T(8,128)(2,1)} %get-tuple-element.26, bf16[3840,1536]{1,0:T(8,128)(2,1)} %all-gather.20.cloned.1.call-done), kind=kOutput, calls=%fused_computation.69 | convolution fusion | flops 18126471168 | bytes 33030144 | tf_op jit(solution)/shard_map/rsd,de->rse/dot_general | solution.py:36
  873.7 14.8 reduce-scatter.20.cloned.1.call-done
  888.6 152.4 %reduce-scatter.18.cloned.1.call-done = f32[192,3840]{1,0:T(8,128)} async-done(((f32[1536,3840]{1,0:T(8,128)}), f32[192,3840]{1,0:T(8,128)}) %reduce-scatter.18.cloned.1.call-update) | async-done | bytes 2949136 | tf_op jit(solution)/shard_map/reduce_scatter | solution.py:64
  1041.0 152.3 %reduce-scatter.16.cloned.1.call-done = f32[192,3840]{1,0:T(8,128)} async-done(((f32[1536,3840]{1,0:T(8,128)}), f32[192,3840]{1,0:T(8,128)}) %reduce-scatter.16.cloned.1.call-update) | async-done | bytes 2949136 | tf_op jit(solution)/shard_map/reduce_scatter | solution.py:64
  1193.2 405.2 %all-reduce.3 = (bf16[192,1024]{1,0:T(8,128)(2,1)}, bf16[192,1024]{1,0:T(8,128)(2,1)}, bf16[192,1024]{1,0:T(8,128)(2,1)}, bf16[128,1536]{1,0:T(8,128)(2,1)}, bf1...) all-reduce(f32[192,1024]{1,0:T(8,128)} %reduce-scatter.8.cloned.1.c, ...), channel_id=1, replica_groups=mesh['dp'=4,'fsdp'=8] {'dp'}, use_global_device_ids=true, to_apply=%region_12.13 | all-reduce | flops 2998272 | bytes 17989632 | tf_op jit(solution)/shard_map/psum | solution.py:65
  (97 shorter events, 1.3 us)
Async XLA Ops:
  7.2 14.6 copy-start
  7.2 8.1 copy-start.16
  7.2 40.9 %all-gather.10.cloned.1.call-start = ((), (), s32[]{:S(2)}) async-start(), calls=%async_computation.8 | async-start | bytes 3538944 | tf_op jit(solution)/shard_map/all_gather | solution.py:60
  7.9 71.0 %all-gather.12.cloned.1.call-start = ((), (), s32[]{:S(2)}) async-start(), calls=%async_computation.9 | async-start | bytes 3538944 | tf_op jit(solution)/shard_map/all_gather | solution.py:60
  8.7 11.7 copy-start.11
  8.7 104.3 %all-gather.8.cloned.1.call-start = ((), (), s32[]{:S(2)}) async-start(), calls=%async_computation.7 | async-start | bytes 3538944 | tf_op jit(solution)/shard_map/all_gather | solution.py:60
  9.4 189.3 %all-gather.14.cloned.1.call-start = ((), (), s32[]{:S(2)}) async-start(), calls=%async_computation.10 | async-start | bytes 3538944 | tf_op jit(solution)/shard_map/all_gather | solution.py:60
  10.0 207.4 %all-gather.20.cloned.1.call-start = ((), (), s32[]{:S(2)}) async-start(), calls=%async_computation.13 | async-start | bytes 13271040 | tf_op jit(solution)/shard_map/all_gather | solution.py:60
  10.6 277.3 %all-gather.18.cloned.1.call-start = ((), (), s32[]{:S(2)}) async-start(), calls=%async_computation.12 | async-start | bytes 13271040 | tf_op jit(solution)/shard_map/all_gather | solution.py:60
  11.2 347.3 %all-gather.16.cloned.1.call-start = ((), (), s32[]{:S(2)}) async-start(), calls=%async_computation.11 | async-start | bytes 13271040 | tf_op jit(solution)/shard_map/all_gather | solution.py:60
  11.9 861.7 %reduce-scatter.14.cloned.1.call-start = ((), (), s32[]{:S(2)}) async-start(), calls=%async_computation.17 | async-start | bytes 7077888 | tf_op jit(solution)/shard_map/reduce_scatter | solution.py:64
  15.3 97.7 %copy-start.20 = (f32[4,384]{1,0:T(4,128)}, f32[4,384]{1,0:T(4,128)S(1)}, u32[]{:S(2)}) copy-start(f32[4,384]{1,0:T(4,128)S(1)} %add_rsqrt_fusion) | copy-start | bytes 18436
  20.4 1.4 copy-start.2
  21.8 26.4 %copy-start.26 = (f32[1536]{0:T(1024)S(1)}, f32[1536]{0:T(1024)}, u32[]{:S(2)}) copy-start(f32[1536]{0:T(1024)} %param.18) | copy-start | bytes 18436
  164.0 23.1 %copy-start.9 = (f32[16,4,384]{2,1,0:T(4,128)}, f32[16,4,384]{2,1,0:T(4,128)S(1)}, u32[]{:S(2)}) copy-start(f32[16,4,384]{2,1,0:T(4,128)S(1)} %get-tuple-element.28) | copy-start | bytes 294916
  164.0 23.1 %copy-start.7 = (bf16[4,384,1024]{1,2,0:T(8,128)(2,1)S(1)}, bf16[4,384,1024]{1,2,0:T(8,128)(2,1)}, u32[]{:S(2)}) copy-start(bf16[4,384,1024]{1,2,0:T(8,128)(2,1)} %copy.54) | copy-start | bytes 9437188
  209.5 0.6 copy-start.14
  210.1 243.1 %copy-start.12 = (f32[4,384]{1,0:T(4,128)}, f32[4,384]{1,0:T(4,128)S(1)}, u32[]{:S(2)}) copy-start(f32[4,384]{1,0:T(4,128)S(1)} %fusion.122) | copy-start | bytes 18436
  210.1 77.8 %copy-start.17 = (f32[1536]{0:T(1024)S(1)}, f32[1536]{0:T(1024)}, u32[]{:S(2)}) copy-start(f32[1536]{0:T(1024)} %param.19) | copy-start | bytes 18436
  424.3 28.8 %copy-start.15 = (f32[4,384]{1,0:T(4,128)S(1)}, f32[4,384]{1,0:T(4,128)}, u32[]{:S(2)}) copy-start(f32[4,384]{1,0:T(4,128)} %copy-done.14) | copy-start | bytes 18436
  453.1 9.4 copy-start.31
  460.3 2.2 copy-start.6
  469.6 1.9 copy-start.25
  469.6 404.1 %reduce-scatter.12.cloned.1.call-start = ((), (), s32[]{:S(2)}) async-start(), calls=%async_computation.16 | async-start | bytes 7077888 | tf_op jit(solution)/shard_map/reduce_scatter | solution.py:64
  480.3 17.4 %slice-start = ((s8[4718592]{0:T(1024)(128)(4,1)}), s8[524288]{0:T(1024)(128)(4,1)S(1)}, s32[]{:S(2)}) async-start(s8[4718592]{0:T(1024)(128)(4,1)} %bitcast.128), calls=%async_computation.21 | async-start | bytes 1048576
  485.4 12.4 slice-start.1
  485.4 12.4 copy-start.21
  485.4 12.4 copy-start.27
  507.5 1.9 copy-start.8
  507.5 1.9 copy-start.10
  507.5 366.2 %reduce-scatter.10.cloned.1.call-start = ((), (), s32[]{:S(2)}) async-start(), calls=%async_computation.15 | async-start | bytes 7077888 | tf_op jit(solution)/shard_map/reduce_scatter | solution.py:64
  535.8 48.7 %copy-start.5 = (bf16[4,384,1024]{1,2,0:T(8,128)(2,1)S(1)}, bf16[4,384,1024]{1,2,0:T(8,128)(2,1)}, u32[]{:S(2)}) copy-start(bf16[4,384,1024]{1,2,0:T(8,128)(2,1)} %copy.55) | copy-start | bytes 9437188
  595.3 1.6 copy-start.29
  607.0 1.9 copy-start.4
  607.0 266.7 %reduce-scatter.8.cloned.1.call-start = ((), (), s32[]{:S(2)}) async-start(), calls=%async_computation.14 | async-start | bytes 7077888 | tf_op jit(solution)/shard_map/reduce_scatter | solution.py:64
  632.2 256.4 %reduce-scatter.20.cloned.1.call-start = ((), (), s32[]{:S(2)}) async-start(), calls=%async_computation.20 | async-start | bytes 26542080 | tf_op jit(solution)/shard_map/reduce_scatter | solution.py:64
  658.2 0.7 copy-start.13
  658.2 0.7 copy-start.18
  658.2 382.7 %reduce-scatter.18.cloned.1.call-start = ((), (), s32[]{:S(2)}) async-start(), calls=%async_computation.19 | async-start | bytes 26542080 | tf_op jit(solution)/shard_map/reduce_scatter | solution.py:64
  686.1 507.1 %reduce-scatter.16.cloned.1.call-start = ((), (), s32[]{:S(2)}) async-start(), calls=%async_computation.18 | async-start | bytes 26542080 | tf_op jit(solution)/shard_map/reduce_scatter | solution.py:64
  713.4 1.9 copy-start.23
  715.3 9.6 copy-start.22
  715.3 9.6 copy-start.30
  715.4 17.3 %slice-start.2 = ((s8[4718592]{0:T(1024)(128)(4,1)}), s8[4194304]{0:T(1024)(128)(4,1)S(1)}, s32[]{:S(2)}) async-start(s8[4718592]{0:T(1024)(128)(4,1)} %bitcast.130), calls=%async_computation.23 | async-start | bytes 8388608
  725.0 7.7 slice-start.3
  725.0 7.7 copy-start.24
  725.0 7.7 copy-start.28
  732.7 12.0 copy-start.3
  744.7 61.2 %copy-start.19 = (f32[1536]{0:T(1024)S(1)}, f32[1536]{0:T(1024)}, u32[]{:S(2)}) copy-start(f32[1536]{0:T(1024)} %get-tuple-element.11) | copy-start | bytes 18436
  847.8 750.7 %copy-start.1 = (f32[32,16]{0,1:T(8,128)S(1)}, f32[32,16]{0,1:T(8,128)}, u32[]{:S(2)}) copy-start(f32[32,16]{0,1:T(8,128)} %param.17) | copy-start | bytes 6148
Sparse Core Ops, SparseCore 0:
  9.9 34.8 all-gather.9
  46.7 32.1 all-gather.11
  80.8 32.1 all-gather.7
  114.8 32.1 all-gather.13
  148.7 68.6 all-gather.19
  219.2 68.6 all-gather.17
  289.8 68.6 all-gather.15
  469.7 61.7 reduce-scatter.13
  534.9 61.7 reduce-scatter.11
  607.1 62.5 reduce-scatter.9
  673.1 61.7 reduce-scatter.7
  738.4 150.1 reduce-scatter.19
  892.2 148.7 reduce-scatter.17
  1044.5 148.7 reduce-scatter.15
where the time goes:
time: 1620 us; the launch traced here: 1610 us
  matrix products  564 us (35%)
  waiting for transfers between devices  458 us (28%)
  blocking collectives  447 us (28%)
  other arithmetic  87.5 us (5%)
  local copies, waits for them, and re-layouts  32.9 us (2%)
    psum x1, blocking collectives, reduce_weight(): return lax.psum(shard, 'dp').astype(jnp.bfloat16)  405 us
    reduce_scatter x7, waiting for transfers between devices, reduce_weight(): shard = lax.psum_scatter(full_grad, 'fsdp', scatter_dimension=0, tiled=True)  320 us
    all_gather x7, waiting for transfers between devices, gather_full(): return lax.all_gather(part, 'fsdp', axis=0, tiled=True)  134 us
    dot_general x7, matrix products, project(): jnp.einsum('rsd,de->rse', tokens_in, weight, preferred_element_type=jnp.f...  131 us
    dot_general x1, matrix products, attn_backward(): jnp.einsum('hrqk,rqkc->ch', d_scores, onehot, precision=lax.Precision.HIG...  61.2 us
    convert_element_type x1, other arithmetic, attn_backward(): d_low = d_scores.astype(jnp.bfloat16)  48.7 us
    psum x1, blocking collectives, local_layer(): lax.psum(d_bias, ROW_AXES)  41.9 us
    sub x1, matrix products, attn_forward(): attn_prob = jax.nn.softmax(scores, axis=-1)  36.7 us
  transfers between devices with their start and end apart: 14, of which 8 were waited for; matrix products, arithmetic and copies ran while one was open for 35% of the time, Pallas kernels for 0%

commit v1 on v0

v1 whole, which is shorter than its diff:
```python
import jax
import jax.numpy as jnp
from jax import lax
from jax.experimental import pallas as pl
from jax.experimental.pallas import tpu as pltpu
from jax.sharding import PartitionSpec as P


EPSILON = 1e-6
NEG_BIG = -1e9
REL_CLASSES = 32
HALF_CLASSES = 16
EXACT_RANGE = 8
THRESHOLDS = (12, 16, 23, 32, 46, 64, 91)
ROW_AXES = ('dp', 'fsdp')
LANES = 128
HEAD_DIM = 64
VMEM_LIMIT = 56 * 1024 * 1024


def rms_norm(values, gain):
    inv_rms = lax.rsqrt(jnp.mean(values * values, axis=-1, keepdims=True) + EPSILON)
    return (values * inv_rms * gain).astype(jnp.bfloat16)


def project(tokens_in, weight):
    return jnp.einsum('td,de->te', tokens_in, weight, preferred_element_type=jnp.float32)


def contract(left, right, left_dim, right_dim):
    return lax.dot_general(left, right, (((left_dim,), (right_dim,)), ((), ())), preferred_element_type=jnp.float32)


def prepare_row(pos_key, pos_query, seg_key, seg_query, cls_ref, mask_ref):
    offset = pos_key[0] - pos_query[0]
    distance = jnp.abs(offset)
    magnitude = jnp.minimum(distance, EXACT_RANGE)
    for bound in THRESHOLDS:
        magnitude = magnitude + jnp.where(distance >= bound, 1, 0)
    cls_ref[...] = magnitude + jnp.where(offset > 0, HALF_CLASSES, 0)
    mask_ref[...] = jnp.where(seg_key[0] == seg_query[0], 0.0, NEG_BIG)


def probabilities(q_head, k_head, head, table, cls_ref, mask_ref):
    seq_len = q_head.shape[0]
    values = jnp.broadcast_to(table[pl.ds(head, 1), :], (seq_len, LANES))
    bias = jnp.concatenate([jnp.take_along_axis(values, cls_ref[:, start:start + LANES], axis=1)
                            for start in range(0, seq_len, LANES)], axis=1)
    scores = contract(k_head, q_head, 1, 1) + bias + mask_ref[...]
    weights = jnp.exp(scores - jnp.max(scores, axis=0, keepdims=True))
    return weights * (1.0 / jnp.sum(weights, axis=0, keepdims=True))


def pair_slice(ref, block):
    return ref[:, pl.ds(pl.multiple_of(block * LANES, LANES), LANES)]


def attn_forward_kernel(pos_key, pos_query, seg_key, seg_query, table, qkv, context, cls_ref, mask_ref):
    prepare_row(pos_key, pos_query, seg_key, seg_query, cls_ref, mask_ref)
    pairs = context.shape[1] // LANES

    @pl.loop(0, pairs)
    def _(pair):
        q_pair, k_pair, v_pair = [pair_slice(qkv, pair + n * pairs) for n in range(3)]
        outs = []
        for sub in range(2):
            lanes = slice(sub * HEAD_DIM, (sub + 1) * HEAD_DIM)
            prob = probabilities(q_pair[:, lanes], k_pair[:, lanes], 2 * pair + sub, table, cls_ref, mask_ref)
            outs.append(contract(v_pair[:, lanes], prob.astype(jnp.bfloat16), 0, 0))
        block = jnp.concatenate(outs, axis=0).T
        context[:, pl.ds(pl.multiple_of(pair * LANES, LANES), LANES)] = block.astype(jnp.bfloat16)


def attn_backward_kernel(pos_key, pos_query, seg_key, seg_query, table, qkv, d_context, *rest):
    d_q, d_k, d_v, d_bias, cls_ref, mask_ref, ds_ref = rest[-7:]
    prepare_row(pos_key, pos_query, seg_key, seg_query, cls_ref, mask_ref)
    pairs = d_context.shape[1] // LANES
    seq_len = d_context.shape[0]

    @pl.when(pl.program_id(0) == 0)
    def _():
        d_bias[...] = jnp.zeros_like(d_bias)

    @pl.loop(0, pairs)
    def _(pair):
        q_pair, k_pair, v_pair = [pair_slice(qkv, pair + n * pairs) for n in range(3)]
        do_pair = pair_slice(d_context, pair)
        dq_parts, dk_parts, dv_parts = [], [], []
        for sub in range(2):
            lanes = slice(sub * HEAD_DIM, (sub + 1) * HEAD_DIM)
            q_head, k_head, v_head, do_head = q_pair[:, lanes], k_pair[:, lanes], v_pair[:, lanes], do_pair[:, lanes]
            head = 2 * pair + sub
            prob = probabilities(q_head, k_head, head, table, cls_ref, mask_ref)
            dv_parts.append(contract(prob.astype(jnp.bfloat16), do_head, 1, 0))
            d_prob = contract(v_head, do_head, 1, 1)
            d_scores = prob * (d_prob - jnp.sum(d_prob * prob, axis=0, keepdims=True))
            ds_ref[head] = d_scores
            d_low = d_scores.astype(jnp.bfloat16)
            dk_parts.append(contract(d_low, q_head, 1, 0))
            dq_parts.append(contract(k_head, d_low, 0, 0))
        out_lanes = pl.ds(pl.multiple_of(pair * LANES, LANES), LANES)
        d_q[:, out_lanes] = jnp.concatenate(dq_parts, axis=0).T.astype(jnp.bfloat16)
        d_k[:, out_lanes] = jnp.concatenate(dk_parts, axis=1).astype(jnp.bfloat16)
        d_v[:, out_lanes] = jnp.concatenate(dv_parts, axis=1).astype(jnp.bfloat16)

    @pl.loop(0, seq_len // 8)
    def _(group):
        keys = pl.ds(pl.multiple_of(group * 8, 8), 8)
        ds_group = ds_ref[:, keys, :].reshape(-1, seq_len)
        high = ds_group.astype(jnp.bfloat16)
        low = (ds_group - high.astype(jnp.float32)).astype(jnp.bfloat16)
        cls_group = jnp.broadcast_to(cls_ref[keys, :][:, None, :], (8, REL_CLASSES, seq_len))
        onehot = jnp.where(cls_group == lax.broadcasted_iota(jnp.int32, cls_group.shape, 1), 1.0, 0.0)
        onehot = onehot.reshape(8 * REL_CLASSES, seq_len).astype(jnp.bfloat16)
        d_bias[...] += contract(high, onehot, 1, 1) + contract(low, onehot, 1, 1)


def attn_specs(seq_len, heads, width, first=0):
    key_spec = pl.BlockSpec((1, seq_len, 1), lambda row: (row + first, 0, 0))
    query_spec = pl.BlockSpec((1, 1, seq_len), lambda row: (row + first, 0, 0))
    table_spec = pl.BlockSpec((heads, LANES), lambda row: (0, 0))
    return [key_spec, query_spec, key_spec, query_spec, table_spec, pl.BlockSpec((seq_len, 3 * width), lambda row: (row + first, 0))]


def attn_cost(rows, seq_len, heads, products):
    scores = rows * heads * seq_len * seq_len
    return pl.CostEstimate(flops=scores * 600 * products, bytes_accessed=rows * seq_len * 8192, transcendentals=scores)


def attn_scratch(seq_len):
    return [pltpu.VMEM((seq_len, seq_len), jnp.int32), pltpu.VMEM((seq_len, seq_len), jnp.float32)]


def attn_forward(index_args, qkv, heads):
    rows, seq_len = index_args[0].shape[:2]
    width = heads * HEAD_DIM
    return pl.pallas_call(
        attn_forward_kernel,
        grid=(rows,),
        in_specs=attn_specs(seq_len, heads, width),
        out_specs=pl.BlockSpec((seq_len, width), lambda row: (row, 0)),
        out_shape=jax.ShapeDtypeStruct((rows * seq_len, width), jnp.bfloat16),
        scratch_shapes=attn_scratch(seq_len),
        cost_estimate=attn_cost(rows, seq_len, heads, 3),
        compiler_params=pltpu.CompilerParams(vmem_limit_bytes=VMEM_LIMIT),
        name='attn_forward',
    )(*index_args, qkv)


def attn_backward(index_args, qkv, d_context, heads, first, count, held):
    rows, seq_len = index_args[0].shape[:2]
    width = heads * HEAD_DIM
    row_spec = pl.BlockSpec((seq_len, width), lambda row: (row + first, 0))
    acc_shape = (8 * heads, 8 * REL_CLASSES)
    d_q, d_k, d_v, sums = pl.pallas_call(
        attn_backward_kernel,
        grid=(count,),
        in_specs=attn_specs(seq_len, heads, width, first) + [row_spec] + [pl.BlockSpec(memory_space=pl.ANY)] * len(held),
        out_specs=[row_spec] * 3 + [pl.BlockSpec(acc_shape, lambda row: (0, 0))],
        out_shape=[jax.ShapeDtypeStruct((rows * seq_len, width), jnp.bfloat16)] * 3 + [jax.ShapeDtypeStruct(acc_shape, jnp.float32)],
        scratch_shapes=attn_scratch(seq_len) + [pltpu.VMEM((heads, seq_len, seq_len), jnp.float32)],
        input_output_aliases={7 + n: n for n in range(len(held))},
        cost_estimate=attn_cost(count, seq_len, heads, 6),
        compiler_params=pltpu.CompilerParams(vmem_limit_bytes=VMEM_LIMIT),
    )(*index_args, qkv, d_context, *held)
    sums = sums.reshape(heads, 8, 8, REL_CLASSES)
    d_bias = sum(sums[:, lane, lane] for lane in range(8))
    return d_q, d_k, d_v, d_bias.T


def gather_full(part):
    return lax.all_gather(part, 'fsdp', axis=0, tiled=True)


def swap_perm(size, bit):
    return [(index, index ^ bit) for index in range(size)]


def swap(value, axis, size, bit):
    return lax.ppermute(value, axis, swap_perm(size, bit))


def widen(value):
    return value.astype(jnp.float32)


def low(value):
    return value.astype(jnp.bfloat16)


def pick(blocks, index):
    return lax.dynamic_index_in_dim(blocks, index, 0, keepdims=False)


class WeightSum:
    def __init__(self, *grads):
        rank = lax.axis_index('fsdp')
        self.core, self.chip, self.plane = rank & 1, rank >> 1, lax.axis_index('dp')
        self.grads = [grad.reshape(4, 2, grad.shape[0] // 8, grad.shape[1]) for grad in grads]
        other = [lax.dynamic_index_in_dim(grad, 1 - self.core, 1, keepdims=False) for grad in self.grads]
        self.sent = jnp.concatenate([low(part) for part in other], axis=-1)

    def cores(self):
        self.got = swap(self.sent, 'fsdp', 8, 1)

    def chip_block(self, chip):
        own = [lax.dynamic_slice(grad, [chip, self.core, 0, 0], (1, 1) + grad.shape[2:])[0, 0] for grad in self.grads]
        return jnp.concatenate(own, axis=-1) + widen(pick(self.got, chip))

    def chips(self):
        self.sends = [low(self.chip_block(self.chip ^ bits)) for bits in (3, 1, 2)]
        self.received = [swap(block, 'fsdp', 8, 2 * bits) for block, bits in zip(self.sends, (3, 1, 2))]

    def planes(self):
        shard = self.chip_block(self.chip)
        for block in self.received:
            shard = shard + widen(block)
        self.shape = shard.shape
        quarters = shard.reshape(4, shard.shape[0] // 4, shard.shape[1])
        self.rings = [[(i, (i + step) % 4) for i in range(4)] for step in (1, 2, 3)]
        self.pieces = [low(pick(quarters, (self.plane + step) % 4)) for step in (1, 2, 3)]
        self.kept = pick(quarters, self.plane)
        self.parts = [lax.ppermute(piece, 'dp', ring) for piece, ring in zip(self.pieces, self.rings)]

    def spread(self):
        self.total = low(self.kept + widen(self.parts[0]) + widen(self.parts[1]) + widen(self.parts[2]))
        self.others = [lax.ppermute(self.total, 'dp', ring) for ring in self.rings]

    def result(self):
        out = jnp.zeros((4,) + self.total.shape, jnp.bfloat16)
        out = lax.dynamic_update_index_in_dim(out, self.total, self.plane, 0)
        for step in (1, 2, 3):
            out = lax.dynamic_update_index_in_dim(out, self.others[step - 1], (self.plane + 4 - step) % 4, 0)
        return out.reshape(self.shape)


def sum_small(value):
    for axis, size, bit in (('dp', 4, 1), ('dp', 4, 2), ('fsdp', 8, 2), ('fsdp', 8, 4)):
        value = value + swap(value, axis, size, bit)
    return value


def after(value, *others):
    return lax.optimization_barrier((value, others))[0]


def token_grad(left, right):
    return jnp.einsum('tk,tn->kn', left, right, preferred_element_type=jnp.float32)


def back_project(grad, weight):
    return jnp.einsum('tn,kn->tk', grad, weight, preferred_element_type=jnp.float32)


def local_layer(x_in, positions, segments, rel_bias, gain_attn, gain_mlp, wq_part, wk_part, wv_part, wo_part, wi0_part, wi1_part, wf_part, grad_out):
    rows, seq_len, dim = x_in.shape
    classes, heads = rel_bias.shape
    width = wq_part.shape[1]
    ff = wi0_part.shape[1]
    w_qkv = gather_full(jnp.concatenate([wq_part, wk_part, wv_part], axis=1))
    w_o = gather_full(wo_part)
    w_i = gather_full(jnp.concatenate([wi0_part, wi1_part], axis=1))
    w_f = gather_full(wf_part)

    tokens = x_in.reshape(rows * seq_len, dim)
    grad_y = grad_out.reshape(rows * seq_len, dim)
    table = jnp.pad(rel_bias.T, ((0, 0), (0, LANES - classes)))
    index_args = (positions[:, :, None], positions[:, None, :], segments[:, :, None], segments[:, None, :], table)
    x_float = widen(tokens)
    normed, norm1_pull = jax.vjp(lambda gain: rms_norm(x_float, gain), gain_attn)
    qkv = low(project(normed, w_qkv))
    context = attn_forward(index_args, qkv, heads)
    hidden = low(x_float + project(context, w_o))
    h_float = widen(hidden)
    mlp_in, norm2_pull = jax.vjp(rms_norm, h_float, gain_mlp)
    w_i = after(w_i, mlp_in)
    gate = project(mlp_in, w_i[:, :ff])
    up_proj = project(mlp_in, w_i[:, ff:])
    act_float, act_pull = jax.vjp(lambda gate_in, up_in: jax.nn.silu(gate_in) * up_in, gate, up_proj)
    hidden_act = low(act_float)

    sum_f = WeightSum(token_grad(hidden_act, grad_y))
    sum_f.cores()
    d_act = low(back_project(after(grad_y, sum_f.sent), w_f))
    d_gate, d_up = act_pull(widen(d_act))
    d_gate, d_up = low(d_gate), low(d_up)
    sum_f.got = after(sum_f.got, d_gate, d_up)
    sum_f.chips()
    d_gate = after(d_gate, sum_f.sends)
    sum_i0 = WeightSum(token_grad(mlp_in, d_gate))
    sum_i0.cores()
    sum_i1 = WeightSum(token_grad(after(mlp_in, sum_i0.sent), d_up))
    sum_i1.cores()
    sum_i0.got = after(sum_i0.got, sum_i1.sent)
    sum_i0.chips()
    sum_f.received = after(sum_f.received, sum_i0.sends)
    sum_f.planes()
    d_mlp_gate = back_project(after(d_gate, sum_f.pieces), w_i[:, :ff])
    sum_i1.got = after(sum_i1.got, d_mlp_gate)
    sum_i1.chips()
    d_up, d_mlp_gate = after([d_up, d_mlp_gate], sum_i1.sends)
    d_mlp_in = low(d_mlp_gate + back_project(d_up, w_i[:, ff:]))
    d_h_norm, d_gain_mlp = norm2_pull(d_mlp_in)
    d_hidden = low(widen(grad_y) + d_h_norm)
    sum_f.parts = after(sum_f.parts, d_hidden)
    sum_f.spread()
    sum_o = WeightSum(token_grad(context, after(d_hidden, sum_f.total)))
    sum_o.cores()
    d_context = low(back_project(after(d_hidden, sum_o.sent), w_o))
    sum_o.got = after(sum_o.got, d_context)
    sum_o.chips()
    d_context = after(d_context, sum_o.sends)
    half = rows // 2
    d_q, d_k, d_v, d_bias = attn_backward(index_args, qkv, d_context, heads, 0, half, ())
    sum_i0.received = after(sum_i0.received, d_q)
    sum_i0.planes()
    d_context = after(d_context, sum_i0.pieces)
    d_q, d_k, d_v, d_bias_rest = attn_backward(index_args, qkv, d_context, heads, half, rows - half, (d_q, d_k, d_v))
    sum_i0.parts, sum_i1.received, sum_o.received, sum_f.others = after(
        [sum_i0.parts, sum_i1.received, sum_o.received, sum_f.others], d_q)
    sum_i1.planes()
    sum_i0.spread()
    d_q, d_k, d_v = after([d_q, d_k, d_v], sum_i1.pieces, sum_i0.total)
    sum_q = WeightSum(*[token_grad(normed, d_part) for d_part in (d_q, d_k, d_v)])
    sum_q.cores()
    d_q = after(d_q, sum_q.sent)
    d_normed_q = back_project(d_q, w_qkv[:, :width])
    sum_q.got = after(sum_q.got, d_normed_q)
    sum_q.chips()
    sum_o.received = after(sum_o.received, sum_q.sends)
    sum_o.planes()
    d_k, d_normed_q = after([d_k, d_normed_q], sum_q.sends, sum_o.pieces)
    d_normed = low(d_normed_q + back_project(d_k, w_qkv[:, width:2 * width]) + back_project(d_v, w_qkv[:, 2 * width:]))
    d_gain_attn = norm1_pull(d_normed)[0]
    sum_i1.parts, sum_o.parts = after([sum_i1.parts, sum_o.parts], d_gain_attn)
    sum_i1.spread()
    sum_o.spread()
    small = jnp.concatenate([(d_bias + d_bias_rest).reshape(-1), d_gain_attn, d_gain_mlp])
    small_swap = swap(small, 'fsdp', 8, 1)
    y_out = low(h_float + project(after(hidden_act, small, sum_i1.total, sum_o.total), w_f)).reshape(x_in.shape)
    sum_q.received, small_swap, sum_i0.others, sum_i1.others, sum_o.others, sum_f.others = after(
        [sum_q.received, small_swap, sum_i0.others, sum_i1.others, sum_o.others, sum_f.others], y_out)
    sum_q.planes()
    small, sum_i0.others, sum_i1.others, sum_o.others, sum_f.others = after(
        [small, sum_i0.others, sum_i1.others, sum_o.others, sum_f.others], sum_q.pieces)
    small = sum_small(small + small_swap)
    d_wf, d_wi0, d_wi1, d_wo = [part.result() for part in (sum_f, sum_i0, sum_i1, sum_o)]
    sum_q.spread()
    d_wqkv = sum_q.result()
    d_wq, d_wk, d_wv = [d_wqkv[:, n * width:(n + 1) * width] for n in range(3)]
    count = classes * heads
    return (y_out, small[:count].reshape(classes, heads), small[count:count + dim], small[count + dim:],
            d_wq, d_wk, d_wv, d_wo, d_wi0, d_wi1, d_wf)


def solution(mesh):
    row_spec = P(ROW_AXES)
    whole = P()
    part_spec = P('fsdp')
    in_specs = (row_spec, row_spec, row_spec, whole, whole, whole) + (part_spec,) * 7 + (row_spec,)
    out_specs = (row_spec, whole, whole, whole) + (part_spec,) * 7
    return jax.shard_map(local_layer, mesh=mesh, in_specs=in_specs, out_specs=out_specs, check_vma=False)
```

time: 1620 us -> 1030 us (0.64)
  blocking collectives: 447 us -> 0 us
  waiting for transfers between devices: 458 us -> 212 us
  matrix products: 564 us -> 346 us
  Pallas kernels: 0 us -> 176 us
  starting transfers between devices: 0.55 us -> 102 us
  local copies, waits for them, and re-layouts: 32.9 us -> 87.6 us
    psum x2 -> x0, blocking collectives: 447 us -> none  [the longest x1 405 us: reduce_weight(): return lax.psum(shard, 'dp').astype(jnp.bfloat16)]
    reduce_scatter x7 -> x0, waiting for transfers between devices: 320 us -> none  [reduce_weight(): shard = lax.psum_scatter(full_grad, 'fsdp', scatter_dimension=0, tiled=True)]
    dot_general x28 -> x19, matrix products: 528 us -> 346 us  [the longest x7 134 us: back_project(): jnp.einsum('tn,kn->tk', grad, weight, preferred_element_type=jnp.float32)]
    pallas_call x0 -> x3, Pallas kernels: none -> 176 us  [the longest x2 128 us: attn_backward(): pl.pallas_call(attn_backward_kernel, grid=(count,), in_specs=attn_specs(s...]
    ppermute x0 -> x55, starting transfers between devices: none -> 102 us  [the longest x15 37.8 us: spread(): self.others = [lax.ppermute(self.total, 'dp', ring) for ring in self.rings]]
    ppermute x0 -> x55, waiting for transfers between devices: none -> 93 us  [the longest x15 48.7 us: spread(): self.others = [lax.ppermute(self.total, 'dp', ring) for ring in self.rings]]
    sub x1 -> x0, matrix products: 36.7 us -> none  [attn_forward(): attn_prob = jax.nn.softmax(scores, axis=-1)]
    convert_element_type x3 -> x8, other arithmetic: 79 us -> 43.9 us  [the longest x6 34.9 us: low(): return value.astype(jnp.bfloat16)]
  transfers between devices with their start and end apart: 14 -> 59, of which waited for: 8 -> 16; matrix products, arithmetic and copies ran while one was open for 35% -> 44% of each run, Pallas kernels for 0% -> 17%
where the time goes in v1:
time: 1030 us; the launch traced here: 1020 us
  matrix products  346 us (34%)
  waiting for transfers between devices  212 us (21%)
  Pallas kernels  176 us (17%)
  starting transfers between devices  102 us (10%)
  local copies, waits for them, and re-layouts  87.6 us (9%)
  other arithmetic  77.2 us (7%)
  between operations  15.3 us (1%)
    dot_general x7, matrix products, back_project(): jnp.einsum('tn,kn->tk', grad, weight, preferred_element_type=jnp.float32)  134 us
    pallas_call x2, Pallas kernels, attn_backward(): pl.pallas_call(attn_backward_kernel, grid=(count,), in_specs=attn_specs(s...  128 us
    all_gather x4, waiting for transfers between devices, gather_full(): return lax.all_gather(part, 'fsdp', axis=0, tiled=True)  117 us
    dot_general x5, matrix products, project(): jnp.einsum('td,de->te', tokens_in, weight, preferred_element_type=jnp.flo...  115 us
    dot_general x7, matrix products, token_grad(): jnp.einsum('tk,tn->kn', left, right, preferred_element_type=jnp.float32)  97.2 us
    ppermute x15, waiting for transfers between devices, spread(): self.others = [lax.ppermute(self.total, 'dp', ring) for ring in self.rings]  48.7 us
    pallas_call x1, Pallas kernels, attn_forward(): pl.pallas_call(attn_forward_kernel, grid=(rows,), in_specs=attn_specs(seq...  48.2 us
    ppermute x25, waiting for transfers between devices, swap(): return lax.ppermute(value, axis, swap_perm(size, bit))  44.2 us
  transfers between devices with their start and end apart: 59, of which 16 were waited for; matrix products, arithmetic and copies ran while one was open for 44% of the time, Pallas kernels for 17%

profile of v1, /device:TPU:0, one launch (start us, length us, event | category | flops | bytes accessed | tf_op | source)
XLA Modules:
  0.0 1016.3 jit_solution(2745752361918425671)
XLA Ops:
  7.2 2.5 pad_maximum_fusion.2
  13.0 3.3 fusion.29
  16.4 5.7 fusion.27
  26.4 45.5 %all-gather.5.cloned.1.call-done = bf16[1536,3072]{1,0:T(8,128)(2,1)} async-done(((bf16[192,3072]{1,0:T(8,128)(2,1)}), bf16[1536,3072]{1,0:T(8,128)(2,1)}) %all-gather.5.cloned.1.call-update) | async-done | bytes 9437200 | tf_op jit(solution)/shard_map/all_gather | solution.py:172
  71.9 20.4 %convolution_convert_fusion.1.qkv = bf16[1536,3072]{1,0:T(8,128)(2,1)} fusion(bf16[1536,1536]{1,0:T(8,128)(2,1)} %fusion.27, bf16[1536,3072]{1,0:T(8,128)(2,1)} %all-gather.5.cloned.1.call-done), kind=kOutput, calls=%fused_computation.29 | convolution fusion | flops 14500233216 | bytes 23592960 | tf_op jit(solution)/shard_map/td,de->te/dot_general | solution.py:27
  92.3 48.2 %attn_forward.1 = bf16[1536,1024]{1,0:T(8,128)(2,1)} custom-call(s32[4,384,1]{2,1,0:T(8,128)} %copy.34.pos_key, s32[4,1,384]{2,1,0:T(1,128)} %broadcast_in_dim.93.pos_query, s32[4,384,1]{2,1,0:T(8,128)} %copy.35.seg_key, s32[4,1,384]{2,1,0:T(1,128)} %broadcast_in_dim.95.seg_query, f32[16,128]{1,0:T(8,128)} %pad.4.table, ...), custom_call_target="tpu_custom_call" | custom-call | flops 16986931200 | bytes 12582912 | tf_op jit(solution)/shard_map/attn_forward/pallas_call | solution.py:137
  140.4 8.7 fusion.23
  151.3 3.2 fusion.19
  154.6 71.9 %all-gather.9.cloned.1.call-done = bf16[1536,7680]{1,0:T(8,128)(2,1)} async-done(((bf16[192,7680]{1,0:T(8,128)(2,1)}), bf16[1536,7680]{1,0:T(8,128)(2,1)}) %all-gather.9.cloned.1.call-update) | async-done | bytes 23592976 | tf_op jit(solution)/shard_map/all_gather | solution.py:172
  226.5 25.8 %fusion.17 = f32[1536,3840]{1,0:T(8,128)} fusion(bf16[1536,1536]{1,0:T(8,128)(2,1)} %fusion.19, bf16[1536,7680]{1,0:T(8,128)(2,1)} %all-gather.9.cloned.1.call-done), kind=kOutput, calls=%fused_computation.38 | convolution fusion | flops 18119393280 | bytes 40108032 | tf_op jit(solution)/shard_map/td,de->te/dot_general | solution.py:27
  252.3 34.7 %fusion.4 = (bf16[3840,1536]{0,1:T(8,128)(2,1)}, f32[1536,3840]{1,0:T(8,128)}) fusion(f32[1536,3840]{1,0:T(8,128)} %fusion.17, bf16[1536,1536]{1,0:T(8,128)(2,1)} %fusion.19, bf16[1536,7680]{1,0:T(8,128)(2,1)} %all-gather.9.cloned.1.call-done), kind=kOutput, calls=%fused_computation.8 | convolution fusion | flops 18154782720 | bytes 75497472 | tf_op jit(solution)/shard_map/td,de->te/dot_general | solution.py:27
  287.0 16.3 %copy.36 = bf16[3840,1536]{1,0:T(8,128)(2,1)} copy(bf16[3840,1536]{0,1:T(8,128)(2,1)} %get-tuple-element.282) | data formatting | bytes 23592960 | tf_op jit(solution)/shard_map/convert_element_type | solution.py:188
  303.3 24.9 %fusion.124 = f32[4,2,480,1536]{3,2,1,0:T(8,128)} fusion(bf16[4,2,480,1536]{3,2,1,0:T(8,128)(2,1)} %bitcast.367, bf16[1536,1536,1,1]{1,0,3,2:T(8,128)(2,1)} %bitcast.376), kind=kOutput, calls=%fused_computation.226 | convolution fusion | flops 18119393280 | bytes 40108032 | tf_op jit(solution)/shard_map/tk,tn->kn/dot_general | solution.py:248
  328.3 7.6 fusion.34
  336.2 43.1 %fusion.3 = (bf16[1536,3840]{1,0:T(8,128)(2,1)}, bf16[1536,3840]{1,0:T(8,128)(2,1)}, bf16[1536,3840]{1,0:T(8,128)(2,1)}) fusion(f32[1536,3840]{1,0:T(8,128)} %fusion.17, f32[1536,3840]{1,0:T(8,128)} %get-tuple-element.283, bf16[1536,1536]{1,0:T(8,128)(2,1)} %bitcast.377, bf16[3840,1536]{1,0:T(8,128)(2,1)} %all-gather.11.cloned.1.call-done), kind=kOutput, calls=%fused_computation.6 | convolution fusion | flops 18225561600 | bytes 99090432 | tf_op jit(solution)/shard_map/tn,kn->tk/dot_general | solution.py:252
  379.3 8.0 fusion.63
  390.8 26.3 %fusion.125 = f32[1536,3840]{1,0:T(8,128)} fusion(bf16[1536,1536]{1,0:T(8,128)(2,1)} %fusion.19, bf16[1536,3840]{1,0:T(8,128)(2,1)} %get-tuple-element.110), kind=kOutput, calls=%fused_computation.227 | convolution fusion | flops 18119393280 | bytes 40108032 | tf_op jit(solution)/shard_map/tk,tn->kn/dot_general | solution.py:248
  417.1 7.4 fusion.35
  424.5 25.1 %fusion.126 = f32[1536,3840]{1,0:T(8,128)} fusion(bf16[1536,1536]{1,0:T(8,128)(2,1)S(1)} %bitcast.384, bf16[1536,3840]{1,0:T(8,128)(2,1)} %get-tuple-element.113), kind=kOutput, calls=%fused_computation.228 | convolution fusion | flops 18119393280 | bytes 40108032 | tf_op jit(solution)/shard_map/tk,tn->kn/dot_general | solution.py:248
  449.6 7.4 fusion.36
  457.7 7.5 fusion.57
  466.9 4.6 fusion.62
  477.9 24.5 %fusion.15 = f32[1536,1536]{1,0:T(8,128)} fusion(bf16[1536,3840]{1,0:T(8,128)(2,1)S(1)} %bitcast.400, bf16[1536,7680]{1,0:T(8,128)(2,1)} %all-gather.9.cloned.1.call-done), kind=kOutput, calls=%fused_computation.36 | convolution fusion | flops 18119393280 | bytes 33030144 | tf_op jit(solution)/shard_map/tn,kn->tk/dot_general | solution.py:252
  502.4 7.3 fusion.54
  509.7 28.4 %fusion.24 = (f32[1536]{0:T(1024)S(1)}, f32[1536]{0:T(1024)}, bf16[1536,1536]{1,0:T(8,128)(2,1)}) fusion(bf16[1536,1536]{1,0:T(8,128)(2,1)} %copy-done, f32[1536]{0:T(1024)S(1)} %copy-done.40, f32[1536]{0:T(1024)S(1)} %copy-done.38, f32[1536,1536]{1,0:T(8,128)} %fusion.15, bf16[1536,3840]{1,0:T(8,128)(2,1)} %get-tuple-element.113, ...), kind=kOutput, calls=%fused_computation.45 | convolution fusion | flops 18142982144 | bytes 42491904 | tf_op jit(solution)/shard_map/tn,kn->tk/dot_general | solution.py:252
  538.1 7.4 fusion.22
  549.0 5.2 fusion.127
  559.4 6.5 convolution_convert_fusion.2.d_context
  567.6 63.9 %shard_map.221 = (bf16[1536,1024]{1,0:T(8,128)(2,1)}, bf16[1536,1024]{1,0:T(8,128)(2,1)}, bf16[1536,1024]{1,0:T(8,128)(2,1)}, f32[128,256]{1,0:T(8,128)}) custom-call(s32[4,384,1]{2,1,0:T(8,128)} %copy.34.pos_key, s32[4,1,384]{2,1,0:T(1,128)} %broadcast_in_dim.93.pos_query, s32[4,384,1]{2,1,0:T(8,128)} %copy.35.seg_key, ...), custom_call_target="tpu_custom_call" | custom-call | flops 16986931200 | bytes 6291456 | tf_op jit(solution)/shard_map/pallas_call | solution.py:155
  634.4 3.0 fusion.53
  637.4 9.4 collective-permute-done.22
  647.9 12.5 %collective-permute-done.23 = bf16[120,1536]{1,0:T(8,128)(2,1)S(1)} collective-permute-done((bf16[120,1536]{1,0:T(8,128)(2,1)}, bf16[120,1536]{1,0:T(8,128)(2,1)S(1)}, u32[]{:S(2)}, u32[]{:S(2)}) %collective-permute-start.23) | collective-permute-done | bytes 368672 | tf_op jit(solution)/shard_map/ppermute | solution.py:227
  661.2 5.3 collective-permute-start.13
  666.5 6.6 copy.57
  673.1 3.3 collective-permute-start.14
  676.4 7.7 collective-permute-done.17
  684.1 2.4 collective-permute-start.19
  687.6 64.1 %shard_map.222 = (bf16[1536,1024]{1,0:T(8,128)(2,1)}, bf16[1536,1024]{1,0:T(8,128)(2,1)}, bf16[1536,1024]{1,0:T(8,128)(2,1)}, f32[128,256]{1,0:T(8,128)}) custom-call(s32[4,384,1]{2,1,0:T(8,128)} %copy.34.pos_key, s32[4,1,384]{2,1,0:T(1,128)} %broadcast_in_dim.93.pos_query, ...), custom_call_target="tpu_custom_call", output_to_operand_aliasing={{0}: (7, {}), {1}: (8, {}), {2}: (9, {})} | custom-call | flops 16986931200 | bytes 6291456 | tf_op jit(solution)/shard_map/pallas_call | solution.py:155
  751.8 4.7 fusion.50
  761.2 5.3 fusion.42
  766.8 3.9 copy-done.52
  770.7 5.1 fusion.46
  775.8 5.3 fusion.44
  797.0 2.7 collective-permute-start.28
  801.7 2.8 dynamic-slice_bitcast_fusion
  804.5 9.3 fusion.40
  813.8 3.7 fusion.70
  822.0 9.5 fusion.38
  831.6 3.0 collective-permute-start.31
  834.5 13.1 %fusion.28 = f32[1536]{0:T(1024)S(1)} fusion(bf16[4,384,1536]{2,1,0:T(8,128)(2,1)S(1)} %bitcast.359, f32[1536]{0:T(1024)S(1)} %copy-done.42, bf16[1536,1024]{1,0:T(8,128)(2,1)} %get-tuple-element.141, bf16[1536,3072]{1,0:T(8,128)(2,1)} %all-gather.5.cloned.1.call-done, f32[1536,1536]{1,0:T(8,128)} %fusion.40, f32[1536,1536]{1,0:T(8,128)} %fusion.38), kind=kOutput, calls=%fused_computation.52 | convolution fusion | flops 4850711040 | bytes 29896704 | tf_op jit(solution)/shard_map/tn,kn->tk/dot_general | solution.py:252
  848.8 2.9 collective-permute-start.38
  856.7 4.4 collective-permute-done.36
  861.1 14.8 %collective-permute-start.43 = (bf16[32,1536]{1,0:T(8,128)(2,1)S(1)}, bf16[32,1536]{1,0:T(8,128)(2,1)S(1)}, u32[]{:S(2)}, u32[]{:S(2)}) collective-permute-start(bf16[32,1536]{1,0:T(8,128)(2,1)S(1)} %get-tuple-element.211), channel_id=1, source_target_pairs={{0,16},{8,24},{16,0},{24,8},{1,17},{9,25},{17,1},{25,9},{2,18},{10... | collective-permute-start | bytes 294920 | tf_op jit(solution)/shard_map/ppermute | solution.py:227
  876.9 9.2 collective-permute-start.44
  887.4 2.4 collective-permute-start.32
  890.5 6.5 collective-permute-done.43
  902.5 25.3 %fusion.33 = bf16[1536,1536]{1,0:T(8,128)(2,1)} fusion(bf16[1536,3840]{1,0:T(8,128)(2,1)} %get-tuple-element.158, bf16[3840,1536]{1,0:T(8,128)(2,1)} %all-gather.11.cloned.1.call-done, bf16[1536,1536]{1,0:T(8,128)(2,1)S(1)} %bitcast.357), kind=kOutput, calls=%fused_computation.57 | convolution fusion | flops 18126471168 | bytes 33030144 | tf_op jit(solution)/shard_map/td,de->te/dot_general | solution.py:27
  927.7 14.1 %collective-permute-done.33 = bf16[192,3072]{1,0:T(8,128)(2,1)S(1)} collective-permute-done((bf16[192,3072]{1,0:T(8,128)(2,1)S(1)}, bf16[192,3072]{1,0:T(8,128)(2,1)S(1)}, u32[]{:S(2)}, u32[]{:S(2)}) %collective-permute-start.33) | collective-permute-done | bytes 1179680 | tf_op jit(solution)/shard_map/ppermute | solution.py:180
  944.2 10.6 %collective-permute-start.50 = (bf16[48,3072]{1,0:T(8,128)(2,1)S(1)}, bf16[48,3072]{1,0:T(8,128)(2,1)S(1)}, u32[]{:S(2)}, u32[]{:S(2)}) collective-permute-start(bf16[48,3072]{1,0:T(8,128)(2,1)S(1)} %get-tuple-element.254), channel_id=1, source_target_pairs={{0,16},{8,24},{16,0},{24,8},{1,17},{9,25},{17,1},{25,9},{2,18},{10... | collective-permute-start | bytes 884744 | tf_op jit(solution)/shard_map/ppermute | solution.py:223
  957.1 10.4 %collective-permute-done.45 = f32[3584]{0:T(1024)S(1)} collective-permute-done((f32[3584]{0:T(1024)S(1)}, f32[3584]{0:T(1024)S(1)}, u32[]{:S(2)}, u32[]{:S(2)}) %collective-permute-start.45) | collective-permute-done | bytes 14368 | tf_op jit(solution)/shard_map/ppermute | solution.py:180
  967.6 6.8 collective-permute-start.46
  974.4 6.9 collective-permute-done.46
  992.3 6.6 collective-permute-done.52
  999.8 8.4 collective-permute-done.53
  (320 shorter events, 98.0 us)
Async XLA Ops:
  7.2 64.7 %all-gather.5.cloned.1.call-start = ((), (), s32[]{:S(2)}) async-start(), calls=%async_computation | async-start | bytes 10616832 | tf_op jit(solution)/shard_map/all_gather | solution.py:172
  9.8 130.7 %all-gather.7.cloned.1.call-start = ((), (), s32[]{:S(2)}) async-start(), calls=%async_computation.1 | async-start | bytes 3538944 | tf_op jit(solution)/shard_map/all_gather | solution.py:172
  10.5 216.0 %all-gather.9.cloned.1.call-start = ((), (), s32[]{:S(2)}) async-start(), calls=%async_computation.2 | async-start | bytes 26542080 | tf_op jit(solution)/shard_map/all_gather | solution.py:172
  12.4 323.8 %all-gather.11.cloned.1.call-start = ((), (), s32[]{:S(2)}) async-start(), calls=%async_computation.3 | async-start | bytes 13271040 | tf_op jit(solution)/shard_map/all_gather | solution.py:172
  335.8 43.5 %collective-permute-start = (bf16[4,480,1536]{2,1,0:T(8,128)(2,1)}, bf16[4,480,1536]{2,1,0:T(8,128)(2,1)}, u32[]{:S(2)}, u32[]{:S(2)}) collective-permute-start(bf16[4,480,1536]{2,1,0:T(8,128)(2,1)} %fusion.34), channel_id=1, source_target_pairs={{0,1},{1,0},{2,3},{3,2},{4,5},{5,4},{6,7},{7,6},{8,9},{9,8},{10,11... | collective-permute-start | bytes 17694728 | tf_op jit(solution)/shard_map/ppermute | solution.py:180
  387.3 77.9 %collective-permute-start.1 = (bf16[480,1536]{1,0:T(8,128)(2,1)}, bf16[480,1536]{1,0:T(8,128)(2,1)S(1)}, u32[]{:S(2)}, u32[]{:S(2)}) collective-permute-start(bf16[480,1536]{1,0:T(8,128)(2,1)} %get-tuple-element.225), channel_id=1, source_target_pairs={{0,6},{1,7},{2,4},{3,5},{4,2},{5,3},{6,0},{7,1},{8,14},{9,15},{10,... | collective-permute-start | bytes 4423688 | tf_op jit(solution)/shard_map/ppermute | solution.py:180
  388.8 76.4 %collective-permute-start.2 = (bf16[480,1536]{1,0:T(8,128)(2,1)}, bf16[480,1536]{1,0:T(8,128)(2,1)S(1)}, u32[]{:S(2)}, u32[]{:S(2)}) collective-permute-start(bf16[480,1536]{1,0:T(8,128)(2,1)} %get-tuple-element.224), channel_id=1, source_target_pairs={{0,2},{1,3},{2,0},{3,1},{4,6},{5,7},{6,4},{7,5},{8,10},{9,11},{10,... | collective-permute-start | bytes 4423688 | tf_op jit(solution)/shard_map/ppermute | solution.py:180
  389.3 76.0 %collective-permute-start.3 = (bf16[480,1536]{1,0:T(8,128)(2,1)}, bf16[480,1536]{1,0:T(8,128)(2,1)}, u32[]{:S(2)}, u32[]{:S(2)}) collective-permute-start(bf16[480,1536]{1,0:T(8,128)(2,1)} %get-tuple-element.223), channel_id=1, source_target_pairs={{0,4},{1,5},{2,6},{3,7},{4,0},{5,1},{6,2},{7,3},{8,12},{9,13},{10,... | collective-permute-start | bytes 4423688 | tf_op jit(solution)/shard_map/ppermute | solution.py:180
  424.5 33.3 %collective-permute-start.4 = (bf16[4,192,3840]{2,1,0:T(8,128)(2,1)}, bf16[4,192,3840]{2,1,0:T(8,128)(2,1)}, u32[]{:S(2)}, u32[]{:S(2)}) collective-permute-start(bf16[4,192,3840]{2,1,0:T(8,128)(2,1)} %fusion.35), channel_id=1, source_target_pairs={{0,1},{1,0},{2,3},{3,2},{4,5},{5,4},{6,7},{7,6},{8,9},{9,8},{10,11... | collective-permute-start | bytes 17694728 | tf_op jit(solution)/shard_map/ppermute | solution.py:180
  457.0 45.4 %collective-permute-start.5 = (bf16[4,192,3840]{2,1,0:T(8,128)(2,1)}, bf16[4,192,3840]{2,1,0:T(8,128)(2,1)}, u32[]{:S(2)}, u32[]{:S(2)}) collective-permute-start(bf16[4,192,3840]{2,1,0:T(8,128)(2,1)} %fusion.36), channel_id=1, source_target_pairs={{0,1},{1,0},{2,3},{3,2},{4,5},{5,4},{6,7},{7,6},{8,9},{9,8},{10,11... | collective-permute-start | bytes 17694728 | tf_op jit(solution)/shard_map/ppermute | solution.py:180
  472.5 73.0 %collective-permute-start.6 = (bf16[120,1536]{1,0:T(8,128)(2,1)}, bf16[120,1536]{1,0:T(8,128)(2,1)}, u32[]{:S(2)}, u32[]{:S(2)}) collective-permute-start(bf16[120,1536]{1,0:T(8,128)(2,1)} %get-tuple-element.252), channel_id=1, source_target_pairs={{0,8},{8,16},{16,24},{24,0},{1,9},{9,17},{17,25},{25,1},{2,10},{10... | collective-permute-start | bytes 1105928 | tf_op jit(solution)/shard_map/ppermute | solution.py:223
  474.0 71.4 %collective-permute-start.7 = (bf16[120,1536]{1,0:T(8,128)(2,1)}, bf16[120,1536]{1,0:T(8,128)(2,1)}, u32[]{:S(2)}, u32[]{:S(2)}) collective-permute-start(bf16[120,1536]{1,0:T(8,128)(2,1)} %get-tuple-element.251), channel_id=1, source_target_pairs={{0,16},{8,24},{16,0},{24,8},{1,17},{9,25},{17,1},{25,9},{2,18},{10... | collective-permute-start | bytes 1105928 | tf_op jit(solution)/shard_map/ppermute | solution.py:223
  476.4 69.1 %collective-permute-start.8 = (bf16[120,1536]{1,0:T(8,128)(2,1)S(1)}, bf16[120,1536]{1,0:T(8,128)(2,1)}, u32[]{:S(2)}, u32[]{:S(2)}) collective-permute-start(bf16[120,1536]{1,0:T(8,128)(2,1)S(1)} %get-tuple-element.250), channel_id=1, source_target_pairs={{0,24},{8,0},{16,8},{24,16},{1,25},{9,1},{17,9},{25,17},{2,26},{10... | collective-permute-start | bytes 1105928 | tf_op jit(solution)/shard_map/ppermute | solution.py:223
  554.4 11.5 %collective-permute-start.9 = (bf16[4,128,1536]{2,1,0:T(8,128)(2,1)S(1)}, bf16[4,128,1536]{2,1,0:T(8,128)(2,1)S(1)}, u32[]{:S(2)}, u32[]{:S(2)}) collective-permute-start(bf16[4,128,1536]{2,1,0:T(8,128)(2,1)S(1)} %fusion.74), channel_id=1, source_target_pairs={{0,1},{1,0},{2,3},{3,2},{4,5},{5,4},{6,7},{7,6},{8,9},{9,8},{10,11... | collective-permute-start | bytes 4718600 | tf_op jit(solution)/shard_map/ppermute | solution.py:180
  554.5 77.1 %collective-permute-start.10 = (bf16[192,3840]{1,0:T(8,128)(2,1)}, bf16[192,3840]{1,0:T(8,128)(2,1)S(1)}, u32[]{:S(2)}, u32[]{:S(2)}) collective-permute-start(bf16[192,3840]{1,0:T(8,128)(2,1)} %get-tuple-element.222), channel_id=1, source_target_pairs={{0,6},{1,7},{2,4},{3,5},{4,2},{5,3},{6,0},{7,1},{8,14},{9,15},{10,... | collective-permute-start | bytes 4423688 | tf_op jit(solution)/shard_map/ppermute | solution.py:180
  555.9 77.4 %collective-permute-start.11 = (bf16[192,3840]{1,0:T(8,128)(2,1)}, bf16[192,3840]{1,0:T(8,128)(2,1)S(1)}, u32[]{:S(2)}, u32[]{:S(2)}) collective-permute-start(bf16[192,3840]{1,0:T(8,128)(2,1)} %get-tuple-element.221), channel_id=1, source_target_pairs={{0,2},{1,3},{2,0},{3,1},{4,6},{5,7},{6,4},{7,5},{8,10},{9,11},{10,... | collective-permute-start | bytes 4423688 | tf_op jit(solution)/shard_map/ppermute | solution.py:180
  556.4 77.4 %collective-permute-start.12 = (bf16[192,3840]{1,0:T(8,128)(2,1)}, bf16[192,3840]{1,0:T(8,128)(2,1)S(1)}, u32[]{:S(2)}, u32[]{:S(2)}) collective-permute-start(bf16[192,3840]{1,0:T(8,128)(2,1)} %get-tuple-element.220), channel_id=1, source_target_pairs={{0,4},{1,5},{2,6},{3,7},{4,0},{5,1},{6,2},{7,3},{8,12},{9,13},{10,... | collective-permute-start | bytes 4423688 | tf_op jit(solution)/shard_map/ppermute | solution.py:180
  558.0 118.4 %collective-permute-start.16 = (bf16[192,3840]{1,0:T(8,128)(2,1)}, bf16[192,3840]{1,0:T(8,128)(2,1)S(1)}, u32[]{:S(2)}, u32[]{:S(2)}) collective-permute-start(bf16[192,3840]{1,0:T(8,128)(2,1)} %get-tuple-element.219), channel_id=1, source_target_pairs={{0,6},{1,7},{2,4},{3,5},{4,2},{5,3},{6,0},{7,1},{8,14},{9,15},{10,... | collective-permute-start | bytes 4423688 | tf_op jit(solution)/shard_map/ppermute | solution.py:180
  565.9 118.2 %collective-permute-start.17 = (bf16[192,3840]{1,0:T(8,128)(2,1)}, bf16[192,3840]{1,0:T(8,128)(2,1)S(1)}, u32[]{:S(2)}, u32[]{:S(2)}) collective-permute-start(bf16[192,3840]{1,0:T(8,128)(2,1)} %get-tuple-element.218), channel_id=1, source_target_pairs={{0,2},{1,3},{2,0},{3,1},{4,6},{5,7},{6,4},{7,5},{8,10},{9,11},{10,... | collective-permute-start | bytes 4423688 | tf_op jit(solution)/shard_map/ppermute | solution.py:180
  631.6 54.9 %collective-permute-start.18 = (bf16[192,3840]{1,0:T(8,128)(2,1)}, bf16[192,3840]{1,0:T(8,128)(2,1)}, u32[]{:S(2)}, u32[]{:S(2)}) collective-permute-start(bf16[192,3840]{1,0:T(8,128)(2,1)} %get-tuple-element.217), channel_id=1, source_target_pairs={{0,4},{1,5},{2,6},{3,7},{4,0},{5,1},{6,2},{7,3},{8,12},{9,13},{10,... | collective-permute-start | bytes 4423688 | tf_op jit(solution)/shard_map/ppermute | solution.py:180
  633.3 13.5 %collective-permute-start.22 = (bf16[120,1536]{1,0:T(8,128)(2,1)}, bf16[120,1536]{1,0:T(8,128)(2,1)S(1)}, u32[]{:S(2)}, u32[]{:S(2)}) collective-permute-start(bf16[120,1536]{1,0:T(8,128)(2,1)} %get-tuple-element.205), channel_id=1, source_target_pairs={{0,8},{8,16},{16,24},{24,0},{1,9},{9,17},{17,25},{25,1},{2,10},{10... | collective-permute-start | bytes 1105928 | tf_op jit(solution)/shard_map/ppermute | solution.py:227
  633.8 26.6 %collective-permute-start.23 = (bf16[120,1536]{1,0:T(8,128)(2,1)}, bf16[120,1536]{1,0:T(8,128)(2,1)S(1)}, u32[]{:S(2)}, u32[]{:S(2)}) collective-permute-start(bf16[120,1536]{1,0:T(8,128)(2,1)} %get-tuple-element.205), channel_id=1, source_target_pairs={{0,16},{8,24},{16,0},{24,8},{1,17},{9,25},{17,1},{25,9},{2,18},{10... | collective-permute-start | bytes 1105928 | tf_op jit(solution)/shard_map/ppermute | solution.py:227
  646.8 26.3 %collective-permute-start.24 = (bf16[120,1536]{1,0:T(8,128)(2,1)}, bf16[120,1536]{1,0:T(8,128)(2,1)}, u32[]{:S(2)}, u32[]{:S(2)}) collective-permute-start(bf16[120,1536]{1,0:T(8,128)(2,1)} %get-tuple-element.205), channel_id=1, source_target_pairs={{0,24},{8,0},{16,8},{24,16},{1,25},{9,1},{17,9},{25,17},{2,26},{10... | collective-permute-start | bytes 1105928 | tf_op jit(solution)/shard_map/ppermute | solution.py:227
  661.2 26.0 %collective-permute-start.13 = (bf16[48,3840]{1,0:T(8,128)(2,1)}, bf16[48,3840]{1,0:T(8,128)(2,1)}, u32[]{:S(2)}, u32[]{:S(2)}) collective-permute-start(bf16[48,3840]{1,0:T(8,128)(2,1)} %get-tuple-element.249), channel_id=1, source_target_pairs={{0,8},{8,16},{16,24},{24,0},{1,9},{9,17},{17,25},{25,1},{2,10},{10... | collective-permute-start | bytes 1105928 | tf_op jit(solution)/shard_map/ppermute | solution.py:223
  673.1 78.6 %collective-permute-start.14 = (bf16[48,3840]{1,0:T(8,128)(2,1)}, bf16[48,3840]{1,0:T(8,128)(2,1)S(1)}, u32[]{:S(2)}, u32[]{:S(2)}) collective-permute-start(bf16[48,3840]{1,0:T(8,128)(2,1)} %get-tuple-element.248), channel_id=1, source_target_pairs={{0,16},{8,24},{16,0},{24,8},{1,17},{9,25},{17,1},{25,9},{2,18},{10... | collective-permute-start | bytes 1105928 | tf_op jit(solution)/shard_map/ppermute | solution.py:223
  676.4 75.3 %copy-start.10 = (bf16[192,3840]{1,0:T(8,128)(2,1)}, bf16[192,3840]{1,0:T(8,128)(2,1)S(1)}, u32[]{:S(2)}) copy-start(bf16[192,3840]{1,0:T(8,128)(2,1)S(1)} %collective-permute-done.16) | copy-start | bytes 4423684
  676.4 75.3 %collective-permute-start.15 = (bf16[48,3840]{1,0:T(8,128)(2,1)}, bf16[48,3840]{1,0:T(8,128)(2,1)S(1)}, u32[]{:S(2)}, u32[]{:S(2)}) collective-permute-start(bf16[48,3840]{1,0:T(8,128)(2,1)} %get-tuple-element.247), channel_id=1, source_target_pairs={{0,24},{8,0},{16,8},{24,16},{1,25},{9,1},{17,9},{25,17},{2,26},{10... | collective-permute-start | bytes 1105928 | tf_op jit(solution)/shard_map/ppermute | solution.py:223
  684.1 67.6 %copy-start.11 = (bf16[192,3840]{1,0:T(8,128)(2,1)}, bf16[192,3840]{1,0:T(8,128)(2,1)S(1)}, u32[]{:S(2)}) copy-start(bf16[192,3840]{1,0:T(8,128)(2,1)S(1)} %collective-permute-done.17) | copy-start | bytes 4423684
  684.1 67.7 %collective-permute-start.19 = (bf16[128,1536]{1,0:T(8,128)(2,1)}, bf16[128,1536]{1,0:T(8,128)(2,1)S(1)}, u32[]{:S(2)}, u32[]{:S(2)}) collective-permute-start(bf16[128,1536]{1,0:T(8,128)(2,1)} %get-tuple-element.228), channel_id=1, source_target_pairs={{0,6},{1,7},{2,4},{3,5},{4,2},{5,3},{6,0},{7,1},{8,14},{9,15},{10,... | collective-permute-start | bytes 1179656 | tf_op jit(solution)/shard_map/ppermute | solution.py:180
  686.5 65.3 %collective-permute-start.20 = (bf16[128,1536]{1,0:T(8,128)(2,1)}, bf16[128,1536]{1,0:T(8,128)(2,1)S(1)}, u32[]{:S(2)}, u32[]{:S(2)}) collective-permute-start(bf16[128,1536]{1,0:T(8,128)(2,1)} %get-tuple-element.227), channel_id=1, source_target_pairs={{0,2},{1,3},{2,0},{3,1},{4,6},{5,7},{6,4},{7,5},{8,10},{9,11},{10,... | collective-permute-start | bytes 1179656 | tf_op jit(solution)/shard_map/ppermute | solution.py:180
  687.2 64.6 %collective-permute-start.21 = (bf16[128,1536]{1,0:T(8,128)(2,1)S(1)}, bf16[128,1536]{1,0:T(8,128)(2,1)S(1)}, u32[]{:S(2)}, u32[]{:S(2)}) collective-permute-start(bf16[128,1536]{1,0:T(8,128)(2,1)S(1)} %get-tuple-element.226), channel_id=1, source_target_pairs={{0,4},{1,5},{2,6},{3,7},{4,0},{5,1},{6,2},{7,3},{8,12},{9,13},{10,... | collective-permute-start | bytes 1179656 | tf_op jit(solution)/shard_map/ppermute | solution.py:180
  786.1 27.7 %collective-permute-start.25 = (bf16[4,192,3072]{2,1,0:T(8,128)(2,1)}, bf16[4,192,3072]{2,1,0:T(8,128)(2,1)}, u32[]{:S(2)}, u32[]{:S(2)}) collective-permute-start(bf16[4,192,3072]{2,1,0:T(8,128)(2,1)} %pad_maximum_fusion), channel_id=1, source_target_pairs={{0,1},{1,0},{2,3},{3,2},{4,5},{5,4},{6,7},{7,6},{8,9},{9,8},{10,11... | collective-permute-start | bytes 14155784 | tf_op jit(solution)/shard_map/ppermute | solution.py:180
  795.8 35.8 %collective-permute-start.26 = (bf16[48,3840]{1,0:T(8,128)(2,1)}, bf16[48,3840]{1,0:T(8,128)(2,1)S(1)}, u32[]{:S(2)}, u32[]{:S(2)}) collective-permute-start(bf16[48,3840]{1,0:T(8,128)(2,1)} %get-tuple-element.246), channel_id=1, source_target_pairs={{0,8},{8,16},{16,24},{24,0},{1,9},{9,17},{17,25},{25,1},{2,10},{10... | collective-permute-start | bytes 1105928 | tf_op jit(solution)/shard_map/ppermute | solution.py:223
  796.5 51.2 %collective-permute-start.27 = (bf16[48,3840]{1,0:T(8,128)(2,1)}, bf16[48,3840]{1,0:T(8,128)(2,1)}, u32[]{:S(2)}, u32[]{:S(2)}) collective-permute-start(bf16[48,3840]{1,0:T(8,128)(2,1)} %get-tuple-element.245), channel_id=1, source_target_pairs={{0,16},{8,24},{16,0},{24,8},{1,17},{9,25},{17,1},{25,9},{2,18},{10... | collective-permute-start | bytes 1105928 | tf_op jit(solution)/shard_map/ppermute | solution.py:223
  797.0 50.8 %collective-permute-start.28 = (bf16[48,3840]{1,0:T(8,128)(2,1)}, bf16[48,3840]{1,0:T(8,128)(2,1)}, u32[]{:S(2)}, u32[]{:S(2)}) collective-permute-start(bf16[48,3840]{1,0:T(8,128)(2,1)} %get-tuple-element.244), channel_id=1, source_target_pairs={{0,24},{8,0},{16,8},{24,16},{1,25},{9,1},{17,9},{25,17},{2,26},{10... | collective-permute-start | bytes 1105928 | tf_op jit(solution)/shard_map/ppermute | solution.py:223
  820.0 28.7 %collective-permute-start.29 = (bf16[32,1536]{1,0:T(8,128)(2,1)}, bf16[32,1536]{1,0:T(8,128)(2,1)S(1)}, u32[]{:S(2)}, u32[]{:S(2)}) collective-permute-start(bf16[32,1536]{1,0:T(8,128)(2,1)} %get-tuple-element.261), channel_id=1, source_target_pairs={{0,8},{8,16},{16,24},{24,0},{1,9},{9,17},{17,25},{25,1},{2,10},{10... | collective-permute-start | bytes 294920 | tf_op jit(solution)/shard_map/ppermute | solution.py:223
  820.6 31.1 %collective-permute-start.30 = (bf16[32,1536]{1,0:T(8,128)(2,1)}, bf16[32,1536]{1,0:T(8,128)(2,1)S(1)}, u32[]{:S(2)}, u32[]{:S(2)}) collective-permute-start(bf16[32,1536]{1,0:T(8,128)(2,1)} %get-tuple-element.260), channel_id=1, source_target_pairs={{0,16},{8,24},{16,0},{24,8},{1,17},{9,25},{17,1},{25,9},{2,18},{10... | collective-permute-start | bytes 294920 | tf_op jit(solution)/shard_map/ppermute | solution.py:223
  822.0 80.4 %slice-start = ((s8[4718592]{0:T(1024)(128)(4,1)}), s8[4194304]{0:T(1024)(128)(4,1)S(1)}, s32[]{:S(2)}) async-start(s8[4718592]{0:T(1024)(128)(4,1)} %bitcast.356), calls=%async_computation.4 | async-start | bytes 8388608
  831.5 70.9 %slice-start.1 = ((s8[4718592]{0:T(1024)(128)(4,1)}), s8[524288]{0:T(1024)(128)(4,1)S(1)}, s32[]{:S(2)}) async-start(s8[4718592]{0:T(1024)(128)(4,1)} %bitcast.356), calls=%async_computation.5 | async-start | bytes 1048576
  831.6 20.1 %collective-permute-start.31 = (bf16[32,1536]{1,0:T(8,128)(2,1)}, bf16[32,1536]{1,0:T(8,128)(2,1)S(1)}, u32[]{:S(2)}, u32[]{:S(2)}) collective-permute-start(bf16[32,1536]{1,0:T(8,128)(2,1)} %get-tuple-element.259), channel_id=1, source_target_pairs={{0,24},{8,0},{16,8},{24,16},{1,25},{9,1},{17,9},{25,17},{2,26},{10... | collective-permute-start | bytes 294920 | tf_op jit(solution)/shard_map/ppermute | solution.py:223
  847.7 13.4 %collective-permute-start.36 = (bf16[48,3840]{1,0:T(8,128)(2,1)S(1)}, bf16[48,3840]{1,0:T(8,128)(2,1)S(1)}, u32[]{:S(2)}, u32[]{:S(2)}) collective-permute-start(bf16[48,3840]{1,0:T(8,128)(2,1)S(1)} %copy-done.35), channel_id=1, source_target_pairs={{0,8},{8,16},{16,24},{24,0},{1,9},{9,17},{17,25},{25,1},{2,10},{10... | collective-permute-start | bytes 1105928 | tf_op jit(solution)/shard_map/ppermute | solution.py:227
  847.8 29.1 %collective-permute-start.37 = (bf16[48,3840]{1,0:T(8,128)(2,1)S(1)}, bf16[48,3840]{1,0:T(8,128)(2,1)S(1)}, u32[]{:S(2)}, u32[]{:S(2)}) collective-permute-start(bf16[48,3840]{1,0:T(8,128)(2,1)S(1)} %copy-done.35), channel_id=1, source_target_pairs={{0,16},{8,24},{16,0},{24,8},{1,17},{9,25},{17,1},{25,9},{2,18},{10... | collective-permute-start | bytes 1105928 | tf_op jit(solution)/shard_map/ppermute | solution.py:227
  848.8 37.4 %collective-permute-start.38 = (bf16[48,3840]{1,0:T(8,128)(2,1)S(1)}, bf16[48,3840]{1,0:T(8,128)(2,1)S(1)}, u32[]{:S(2)}, u32[]{:S(2)}) collective-permute-start(bf16[48,3840]{1,0:T(8,128)(2,1)S(1)} %copy-done.35), channel_id=1, source_target_pairs={{0,24},{8,0},{16,8},{24,16},{1,25},{9,1},{17,9},{25,17},{2,26},{10... | collective-permute-start | bytes 1105928 | tf_op jit(solution)/shard_map/ppermute | solution.py:227
  853.0 47.2 %collective-permute-start.39 = (bf16[48,3840]{1,0:T(8,128)(2,1)S(1)}, bf16[48,3840]{1,0:T(8,128)(2,1)S(1)}, u32[]{:S(2)}, u32[]{:S(2)}) collective-permute-start(bf16[48,3840]{1,0:T(8,128)(2,1)S(1)} %get-tuple-element.207), channel_id=1, source_target_pairs={{0,8},{8,16},{16,24},{24,0},{1,9},{9,17},{17,25},{25,1},{2,10},{10... | collective-permute-start | bytes 1105928 | tf_op jit(solution)/shard_map/ppermute | solution.py:227
  854.6 35.2 %collective-permute-start.42 = (bf16[32,1536]{1,0:T(8,128)(2,1)S(1)}, bf16[32,1536]{1,0:T(8,128)(2,1)S(1)}, u32[]{:S(2)}, u32[]{:S(2)}) collective-permute-start(bf16[32,1536]{1,0:T(8,128)(2,1)S(1)} %get-tuple-element.211), channel_id=1, source_target_pairs={{0,8},{8,16},{16,24},{24,0},{1,9},{9,17},{17,25},{25,1},{2,10},{10... | collective-permute-start | bytes 294920 | tf_op jit(solution)/shard_map/ppermute | solution.py:227
  861.1 35.8 %collective-permute-start.43 = (bf16[32,1536]{1,0:T(8,128)(2,1)S(1)}, bf16[32,1536]{1,0:T(8,128)(2,1)S(1)}, u32[]{:S(2)}, u32[]{:S(2)}) collective-permute-start(bf16[32,1536]{1,0:T(8,128)(2,1)S(1)} %get-tuple-element.211), channel_id=1, source_target_pairs={{0,16},{8,24},{16,0},{24,8},{1,17},{9,25},{17,1},{25,9},{2,18},{10... | collective-permute-start | bytes 294920 | tf_op jit(solution)/shard_map/ppermute | solution.py:227
  876.9 21.6 %collective-permute-start.44 = (bf16[32,1536]{1,0:T(8,128)(2,1)S(1)}, bf16[32,1536]{1,0:T(8,128)(2,1)S(1)}, u32[]{:S(2)}, u32[]{:S(2)}) collective-permute-start(bf16[32,1536]{1,0:T(8,128)(2,1)S(1)} %get-tuple-element.211), channel_id=1, source_target_pairs={{0,24},{8,0},{16,8},{24,16},{1,25},{9,1},{17,9},{25,17},{2,26},{10... | collective-permute-start | bytes 294920 | tf_op jit(solution)/shard_map/ppermute | solution.py:227
  886.1 1.2 collective-permute-start.35
  887.4 40.3 %collective-permute-start.32 = (bf16[192,3072]{1,0:T(8,128)(2,1)S(1)}, bf16[192,3072]{1,0:T(8,128)(2,1)S(1)}, u32[]{:S(2)}, u32[]{:S(2)}) collective-permute-start(bf16[192,3072]{1,0:T(8,128)(2,1)S(1)} %copy-done.23), channel_id=1, source_target_pairs={{0,6},{1,7},{2,4},{3,5},{4,2},{5,3},{6,0},{7,1},{8,14},{9,15},{10,... | collective-permute-start | bytes 3538952 | tf_op jit(solution)/shard_map/ppermute | solution.py:180
  889.8 52.0 %collective-permute-start.33 = (bf16[192,3072]{1,0:T(8,128)(2,1)S(1)}, bf16[192,3072]{1,0:T(8,128)(2,1)S(1)}, u32[]{:S(2)}, u32[]{:S(2)}) collective-permute-start(bf16[192,3072]{1,0:T(8,128)(2,1)S(1)} %copy-done.22), channel_id=1, source_target_pairs={{0,2},{1,3},{2,0},{3,1},{4,6},{5,7},{6,4},{7,5},{8,10},{9,11},{10,... | collective-permute-start | bytes 3538952 | tf_op jit(solution)/shard_map/ppermute | solution.py:180
  896.9 44.9 %collective-permute-start.34 = (bf16[192,3072]{1,0:T(8,128)(2,1)S(1)}, bf16[192,3072]{1,0:T(8,128)(2,1)S(1)}, u32[]{:S(2)}, u32[]{:S(2)}) collective-permute-start(bf16[192,3072]{1,0:T(8,128)(2,1)S(1)} %copy-done.21), channel_id=1, source_target_pairs={{0,4},{1,5},{2,6},{3,7},{4,0},{5,1},{6,2},{7,3},{8,12},{9,13},{10,... | collective-permute-start | bytes 3538952 | tf_op jit(solution)/shard_map/ppermute | solution.py:180
  898.6 29.1 %collective-permute-start.40 = (bf16[48,3840]{1,0:T(8,128)(2,1)S(1)}, bf16[48,3840]{1,0:T(8,128)(2,1)S(1)}, u32[]{:S(2)}, u32[]{:S(2)}) collective-permute-start(bf16[48,3840]{1,0:T(8,128)(2,1)S(1)} %get-tuple-element.207), channel_id=1, source_target_pairs={{0,16},{8,24},{16,0},{24,8},{1,17},{9,25},{17,1},{25,9},{2,18},{10... | collective-permute-start | bytes 1105928 | tf_op jit(solution)/shard_map/ppermute | solution.py:227
  900.3 27.4 %collective-permute-start.41 = (bf16[48,3840]{1,0:T(8,128)(2,1)S(1)}, bf16[48,3840]{1,0:T(8,128)(2,1)S(1)}, u32[]{:S(2)}, u32[]{:S(2)}) collective-permute-start(bf16[48,3840]{1,0:T(8,128)(2,1)S(1)} %get-tuple-element.207), channel_id=1, source_target_pairs={{0,24},{8,0},{16,8},{24,16},{1,25},{9,1},{17,9},{25,17},{2,26},{10... | collective-permute-start | bytes 1105928 | tf_op jit(solution)/shard_map/ppermute | solution.py:227
  944.2 42.4 %collective-permute-start.51 = (bf16[48,3072]{1,0:T(8,128)(2,1)S(1)}, bf16[48,3072]{1,0:T(8,128)(2,1)S(1)}, u32[]{:S(2)}, u32[]{:S(2)}) collective-permute-start(bf16[48,3072]{1,0:T(8,128)(2,1)S(1)} %get-tuple-element.253), channel_id=1, source_target_pairs={{0,24},{8,0},{16,8},{24,16},{1,25},{9,1},{17,9},{25,17},{2,26},{10... | collective-permute-start | bytes 884744 | tf_op jit(solution)/shard_map/ppermute | solution.py:223
  944.2 42.4 %collective-permute-start.50 = (bf16[48,3072]{1,0:T(8,128)(2,1)S(1)}, bf16[48,3072]{1,0:T(8,128)(2,1)S(1)}, u32[]{:S(2)}, u32[]{:S(2)}) collective-permute-start(bf16[48,3072]{1,0:T(8,128)(2,1)S(1)} %get-tuple-element.254), channel_id=1, source_target_pairs={{0,16},{8,24},{16,0},{24,8},{1,17},{9,25},{17,1},{25,9},{2,18},{10... | collective-permute-start | bytes 884744 | tf_op jit(solution)/shard_map/ppermute | solution.py:223
  954.9 31.7 %collective-permute-start.49 = (bf16[48,3072]{1,0:T(8,128)(2,1)S(1)}, bf16[48,3072]{1,0:T(8,128)(2,1)S(1)}, u32[]{:S(2)}, u32[]{:S(2)}) collective-permute-start(bf16[48,3072]{1,0:T(8,128)(2,1)S(1)} %get-tuple-element.255), channel_id=1, source_target_pairs={{0,8},{8,16},{16,24},{24,0},{1,9},{9,17},{17,25},{25,1},{2,10},{10... | collective-permute-start | bytes 884744 | tf_op jit(solution)/shard_map/ppermute | solution.py:223
  954.9 12.7 %collective-permute-start.45 = (f32[3584]{0:T(1024)S(1)}, f32[3584]{0:T(1024)S(1)}, u32[]{:S(2)}, u32[]{:S(2)}) collective-permute-start(f32[3584]{0:T(1024)S(1)} %add.604), channel_id=1, source_target_pairs={{0,8},{8,0},{16,24},{24,16},{1,9},{9,1},{17,25},{25,17},{2,10},{10... | collective-permute-start | bytes 43016 | tf_op jit(solution)/shard_map/ppermute | solution.py:180
  957.1 52.2 %copy-start.16 = (bf16[4,120,1536]{2,1,0:T(8,128)(2,1)}, bf16[4,120,1536]{2,1,0:T(8,128)(2,1)S(1)}, u32[]{:S(2)}) copy-start(bf16[4,120,1536]{2,1,0:T(8,128)(2,1)S(1)} %bitcast_dynamic-update-slice_fusion) | copy-start | bytes 4423684
  967.6 13.7 %collective-permute-start.46 = (f32[3584]{0:T(1024)S(1)}, f32[3584]{0:T(1024)S(1)}, u32[]{:S(2)}, u32[]{:S(2)}) collective-permute-start(f32[3584]{0:T(1024)S(1)} %add.605), channel_id=1, source_target_pairs={{0,16},{8,24},{16,0},{24,8},{1,17},{9,25},{17,1},{25,9},{2,18},{10... | collective-permute-start | bytes 43016 | tf_op jit(solution)/shard_map/ppermute | solution.py:180
  981.3 3.7 collective-permute-start.47
  985.0 3.7 collective-permute-start.48
  987.0 11.9 %collective-permute-start.52 = (bf16[48,3072]{1,0:T(8,128)(2,1)S(1)}, bf16[48,3072]{1,0:T(8,128)(2,1)}, u32[]{:S(2)}, u32[]{:S(2)}) collective-permute-start(bf16[48,3072]{1,0:T(8,128)(2,1)S(1)} %get-tuple-element.213), channel_id=1, source_target_pairs={{0,8},{8,16},{16,24},{24,0},{1,9},{9,17},{17,25},{25,1},{2,10},{10... | collective-permute-start | bytes 884744 | tf_op jit(solution)/shard_map/ppermute | solution.py:227
  990.1 18.1 %collective-permute-start.53 = (bf16[48,3072]{1,0:T(8,128)(2,1)S(1)}, bf16[48,3072]{1,0:T(8,128)(2,1)S(1)}, u32[]{:S(2)}, u32[]{:S(2)}) collective-permute-start(bf16[48,3072]{1,0:T(8,128)(2,1)S(1)} %get-tuple-element.213), channel_id=1, source_target_pairs={{0,16},{8,24},{16,0},{24,8},{1,17},{9,25},{17,1},{25,9},{2,18},{10... | collective-permute-start | bytes 884744 | tf_op jit(solution)/shard_map/ppermute | solution.py:227
  990.1 18.1 %collective-permute-start.54 = (bf16[48,3072]{1,0:T(8,128)(2,1)S(1)}, bf16[48,3072]{1,0:T(8,128)(2,1)S(1)}, u32[]{:S(2)}, u32[]{:S(2)}) collective-permute-start(bf16[48,3072]{1,0:T(8,128)(2,1)S(1)} %get-tuple-element.213), channel_id=1, source_target_pairs={{0,24},{8,0},{16,8},{24,16},{1,25},{9,1},{17,9},{25,17},{2,26},{10... | collective-permute-start | bytes 884744 | tf_op jit(solution)/shard_map/ppermute | solution.py:227
  (63 other events, 722.7 us)
Sparse Core Ops, SparseCore 0:
  10.5 61.4 all-gather.4
  73.8 32.1 all-gather.6
  107.9 118.5 all-gather.8
  228.2 68.6 all-gather.10
